TPU v7x, 256 devices: a whole 4x4x8 slice. The times are simulated.
256 devices in a mesh: grp: 8 (over y_hi, x), slab: 32 (over z, y_lo, core).
Axes of the slice: x: 4, y: 4 (y_hi: 2, y_lo: 2; y = y_hi * 2 + y_lo), z: 8, core: 2. Of those that a mesh axis runs over, the one named last changes fastest.
Arguments:
- source: float32 [256, 32, 4096], P('grp', None, 'slab'), may hold values from -6 to 6
- occupancy: int32 [32, 4, 512], P('grp', None, 'slab'), may hold values 0 or 1
- classes: int32 [32, 4, 512], P('grp', None, 'slab'), may hold values from 0 to 15
- screen_table: float32 [16], replicated, may hold values from 0.5 to 8
- parents: int32 [16, 2, 256], P('grp', None, 'slab'), may hold values from 0 to 127, as said below
- coarse: float32 [8, 128, 512], P('grp', 'slab'), may hold values from -6 to 6
Outputs:
- middle_field: float32 [128, 16, 2048], P('grp', None, 'slab')
- finest_field: float32 [256, 32, 4096], P('grp', None, 'slab')
Inputs may be any that keep to these rules, and one draw needn't show every extreme that they name: parents[I, J, K] is the position, in the list of the group that holds the brick, of the depth-12 brick containing depth-13 brick (I, J, K); each group's list holds each depth-12 brick of the group's region once, so each position is the parent of eight depth-13 bricks. The parent of a brick on slab index s lies in list positions [(s - 1) * 4, (s + 2) * 4).
All inputs are finite; a program needn't handle non-finite values. No bound on the sum of `occupancy` on one device may be relied on, other than what follows from the above.
Results may differ from a plain program's by a relative error of at most 0.00002.
Values sent between devices are 32-bit elements; how exact they have to be, the bound alone decides.
No kernel may reach another device: no remote copies, remote signals or barrier semaphores. Data moves between devices by JAX's collectives and lax.ppermute only.
A program may use at most 128 MiB of HBM per device.

v0:
```python
import jax
import jax.numpy as jnp
from jax import lax
from jax.sharding import PartitionSpec as P

BRICK = 8
SWEEPS = 3


screen_strength = 4.0
relaxation = 2.0 / 3.0
stiff_diagonal = 8.0 / 3.0
mass_diagonal = 8.0 / 27.0


def extended(block, sides, width):
    for axis, dim in sides:
        count = lax.axis_size(axis)
        forward = [(i, i + 1) for i in range(count - 1)]
        backward = [(target, source) for source, target in forward]
        low = lax.ppermute(
            lax.slice_in_dim(block, block.shape[dim] - width, None, axis=dim), axis, forward
        )
        high = lax.ppermute(lax.slice_in_dim(block, 0, width, axis=dim), axis, backward)
        block = jnp.concatenate([low, block, high], axis=dim)
    return block


def expand(values, factor):
    first, second, third = values.shape
    wide = jnp.broadcast_to(
        values[:, None, :, None, :, None], (first, factor, second, factor, third, factor)
    )
    return wide.reshape(first * factor, second * factor, third * factor)


def mass_along(values, along):
    length = values.shape[along]
    lower = lax.slice_in_dim(values, 0, length - 2, axis=along)
    middle = lax.slice_in_dim(values, 1, length - 1, axis=along)
    upper = lax.slice_in_dim(values, 2, length, axis=along)
    return (lower + 4.0 * middle + upper) / 6.0


def stiff_along(values, along):
    length = values.shape[along]
    lower = lax.slice_in_dim(values, 0, length - 2, axis=along)
    middle = lax.slice_in_dim(values, 1, length - 1, axis=along)
    upper = lax.slice_in_dim(values, 2, length, axis=along)
    return 2.0 * middle - lower - upper


def relax_step(padded, source, inverse, screen):
    padded_all = jnp.pad(padded, ((0, 0), (1, 1), (0, 0)))
    mass_z = mass_along(padded_all, 2)
    stiff_z = stiff_along(padded_all, 2)
    mass_yz = mass_along(mass_z, 1)
    mixed = stiff_along(mass_z, 1) + mass_along(stiff_z, 1)
    laplace = stiff_along(mass_yz, 0) + mass_along(mixed, 0)
    mass_all = mass_along(mass_yz, 0)
    center = padded[1:-1, :, 1:-1]
    return center + relaxation * inverse * (source - laplace - screen * mass_all)


def smooth(field, source, inverse_brick, screen_brick, spread):
    inverse = expand(inverse_brick, spread)
    screen = expand(screen_brick, spread)
    for sweep_index in range(SWEEPS):
        padded = extended(field, (("grp", 0), ("slab", 2)), 1)
        field = relax_step(padded, source, inverse, screen)
    return field


def lift(brick_rows, count_x, count_y, count_z):
    half = BRICK // 2
    cells = brick_rows.reshape(count_x, count_y, count_z, 2, half, 2, half, 2, half)
    pairs = jnp.arange(2, dtype=jnp.int32)
    pick_x = ((jnp.arange(count_x, dtype=jnp.int32) % 2)[:, None] == pairs).astype(jnp.float32)
    pick_y = ((jnp.arange(count_y, dtype=jnp.int32) % 2)[:, None] == pairs).astype(jnp.float32)
    pick_z = ((jnp.arange(count_z, dtype=jnp.int32) % 2)[:, None] == pairs).astype(jnp.float32)
    chosen = jnp.sum(cells * pick_x[:, None, None, :, None, None, None, None, None], axis=3)
    chosen = jnp.sum(chosen * pick_y[None, :, None, None, :, None, None, None], axis=4)
    chosen = jnp.sum(chosen * pick_z[None, None, :, None, None, :, None], axis=5)
    fine = jnp.broadcast_to(
        chosen[:, :, :, :, None, :, None, :, None],
        (count_x, count_y, count_z, half, 2, half, 2, half, 2),
    )
    fine = fine.reshape(count_x, count_y, count_z, BRICK, BRICK, BRICK)
    return fine.transpose(0, 3, 1, 4, 2, 5).reshape(
        count_x * BRICK, count_y * BRICK, count_z * BRICK
    )


def local(source, occupancy, classes, screen_table, parents, coarse):
    shard_len = coarse.shape[1]
    neighbours = extended(coarse, (("slab", 1),), shard_len)
    offset = (lax.axis_index("slab") - 1) * shard_len
    position = (parents - offset).reshape(-1)
    brick_rows = jnp.take(neighbours[0], position, axis=0)
    occupied = occupancy.astype(jnp.float32)
    labels = jnp.arange(screen_table.shape[0], dtype=jnp.int32)
    weight = jnp.sum(jnp.where(classes[..., None] == labels, screen_table, 0.0), axis=-1)
    screen_brick = screen_strength * weight
    inverse_brick = occupied / (stiff_diagonal + screen_brick * mass_diagonal)
    count_x, count_y, count_z = parents.shape
    middle_field = lift(brick_rows, count_x, count_y, count_z) * expand(occupied, BRICK // 2)
    size_x, size_y, size_z = source.shape
    source_mid = 0.25 * source.reshape(size_x // 2, 2, size_y // 2, 2, size_z // 2, 2).sum(
        axis=(1, 3, 5)
    )
    middle_field = smooth(middle_field, source_mid, inverse_brick, screen_brick, BRICK // 2)
    finest_field = expand(middle_field, 2) * expand(occupied, BRICK)
    finest_field = smooth(finest_field, source, inverse_brick, screen_brick, BRICK)
    return (middle_field, finest_field)


def solution(mesh):
    placed = (
        P("grp", None, "slab"),
        P("grp", None, "slab"),
        P("grp", None, "slab"),
        P(),
        P("grp", None, "slab"),
        P("grp", "slab", None),
    )
    return jax.shard_map(
        local,
        mesh=mesh,
        in_specs=placed,
        out_specs=(P("grp", None, "slab"), P("grp", None, "slab")),
        check_vma=False,
    )
```

profile of v0, /device:TPU:111, one launch (start us, length us, event | category | flops | bytes accessed | tf_op | source)
XLA Modules:
  0.0 283.7 jit_solution(17707387337939636701)
XLA Ops:
  0.6 5.2 %collective-permute-start = (f32[1,4,512]{2,1,0:T(4,128)}, f32[1,4,512]{2,1,0:T(4,128)S(1)}, u32[]{:S(2)}, u32[]{:S(2)}) collective-permute-start(f32[1,4,512]{2,1,0:T(4,128)} %param.11), channel_id=1, source_target_pairs={{0,1},{1,2},{2,3},{3,4},{4,5},{5,6},{6,7},{7,8},{8,9},{9,10},{10,1... | collective-permute-start | bytes 24584 | tf_op jit(solution)/shard_map/ppermute | solution.py:21
  5.8 1.9 collective-permute-start.1
  10.6 2.5 collective-permute-done.1
  17.4 4.1 %collective-permute-start.2 = (f32[1,16,64]{2,1,0:T(8,128)S(1)}, f32[1,16,64]{2,1,0:T(8,128)S(1)}, u32[]{:S(2)}, u32[]{:S(2)}) collective-permute-start(f32[1,16,64]{2,1,0:T(8,128)S(1)} %get-tuple-element.50), channel_id=1, source_target_pairs={{0,32},{32,64},{64,96},{96,128},{128,160},{160,192},{192,224},{1,3... | collective-permute-start | bytes 12296 | tf_op jit(solution)/shard_map/ppermute | solution.py:21
  21.6 1.9 collective-permute-start.3
  23.7 5.9 %collective-permute-done.3 = f32[1,16,64]{2,1,0:T(8,128)S(1)} collective-permute-done((f32[1,16,64]{2,1,0:T(8,128)S(1)}, f32[1,16,64]{2,1,0:T(8,128)S(1)}, u32[]{:S(2)}, u32[]{:S(2)}) %collective-permute-start.3) | collective-permute-done | bytes 4128 | tf_op jit(solution)/shard_map/ppermute | solution.py:24
  29.8 5.2 %collective-permute-start.4 = (f32[18,16,1]{2,1,0:T(8,128)S(1)}, f32[18,16,1]{2,1,0:T(8,128)S(1)}, u32[]{:S(2)}, u32[]{:S(2)}) collective-permute-start(f32[18,16,1]{2,1,0:T(8,128)S(1)} %get-tuple-element.44), channel_id=1, source_target_pairs={{0,1},{1,2},{2,3},{3,4},{4,5},{5,6},{6,7},{7,8},{8,9},{9,10},{10,1... | collective-permute-start | bytes 3464 | tf_op jit(solution)/shard_map/ppermute | solution.py:21
  35.0 1.9 collective-permute-start.5
  39.8 2.7 reshape.173
  42.6 34.9 %reshape.172 = f32[16,2,16,2,64,2]{5,4,3,2,1,0:T(8,128)} reshape(f32[32,32,128]{2,1,0:T(8,128)S(1)} %copy-done) | data formatting | bytes 1048576 | tf_op jit(solution)/shard_map/reshape | solution.py:108
  77.4 12.2 %reduce_sum.49 = f32[16,16,64]{2,1,0:T(8,128)S(1)} reduce(f32[16,2,16,2,64,2]{5,4,3,2,1,0:T(8,128)} %reshape.172, f32[]{:T(128)} %constant.110.clone.1), dimensions={1,3,5}, to_apply=%region_4.5 | reduce | flops 114688 | bytes 589828 | tf_op jit(solution)/shard_map/reduce_sum | solution.py:108
  90.3 1.9 collective-permute-start.6
  92.2 3.4 %collective-permute-start.7 = (f32[1,16,64]{2,1,0:T(8,128)S(1)}, f32[1,16,64]{2,1,0:T(8,128)S(1)}, u32[]{:S(2)}, u32[]{:S(2)}) collective-permute-start(f32[1,16,64]{2,1,0:T(8,128)S(1)} %get-tuple-element.49), channel_id=1, source_target_pairs={{32,0},{64,32},{96,64},{128,96},{160,128},{192,160},{224,192},{33,... | collective-permute-start | bytes 12296 | tf_op jit(solution)/shard_map/ppermute | solution.py:24
  95.6 4.6 %collective-permute-done.7 = f32[1,16,64]{2,1,0:T(8,128)S(1)} collective-permute-done((f32[1,16,64]{2,1,0:T(8,128)S(1)}, f32[1,16,64]{2,1,0:T(8,128)S(1)}, u32[]{:S(2)}, u32[]{:S(2)}) %collective-permute-start.7) | collective-permute-done | bytes 4128 | tf_op jit(solution)/shard_map/ppermute | solution.py:24
  100.3 7.0 %collective-permute-start.8 = (f32[18,16,1]{2,1,0:T(8,128)S(1)}, f32[18,16,1]{2,1,0:T(8,128)S(1)}, u32[]{:S(2)}, u32[]{:S(2)}) collective-permute-start(f32[18,16,1]{2,1,0:T(8,128)S(1)} %get-tuple-element.42), channel_id=1, source_target_pairs={{0,1},{1,2},{2,3},{3,4},{4,5},{5,6},{6,7},{7,8},{8,9},{9,10},{10,1... | collective-permute-start | bytes 3464 | tf_op jit(solution)/shard_map/ppermute | solution.py:21
  107.3 1.9 collective-permute-start.9
  109.4 6.5 %collective-permute-done.9 = f32[18,16,1]{2,1,0:T(8,128)S(1)} collective-permute-done((f32[18,16,1]{2,1,0:T(8,128)S(1)}, f32[18,16,1]{2,1,0:T(8,128)S(1)}, u32[]{:S(2)}, u32[]{:S(2)}) %collective-permute-start.9) | collective-permute-done | bytes 1184 | tf_op jit(solution)/shard_map/ppermute | solution.py:24
  116.5 1.9 collective-permute-start.10
  118.4 3.4 %collective-permute-start.11 = (f32[1,16,64]{2,1,0:T(8,128)S(1)}, f32[1,16,64]{2,1,0:T(8,128)S(1)}, u32[]{:S(2)}, u32[]{:S(2)}) collective-permute-start(f32[1,16,64]{2,1,0:T(8,128)S(1)} %get-tuple-element.47), channel_id=1, source_target_pairs={{32,0},{64,32},{96,64},{128,96},{160,128},{192,160},{224,192},{33,... | collective-permute-start | bytes 12296 | tf_op jit(solution)/shard_map/ppermute | solution.py:24
  121.8 4.6 %collective-permute-done.11 = f32[1,16,64]{2,1,0:T(8,128)S(1)} collective-permute-done((f32[1,16,64]{2,1,0:T(8,128)S(1)}, f32[1,16,64]{2,1,0:T(8,128)S(1)}, u32[]{:S(2)}, u32[]{:S(2)}) %collective-permute-start.11) | collective-permute-done | bytes 4128 | tf_op jit(solution)/shard_map/ppermute | solution.py:24
  126.5 2.9 %collective-permute-start.12 = (f32[18,16,1]{2,1,0:T(8,128)S(1)}, f32[18,16,1]{2,1,0:T(8,128)S(1)}, u32[]{:S(2)}, u32[]{:S(2)}) collective-permute-start(f32[18,16,1]{2,1,0:T(8,128)S(1)} %get-tuple-element.40), channel_id=1, source_target_pairs={{0,1},{1,2},{2,3},{3,4},{4,5},{5,6},{6,7},{7,8},{8,9},{9,10},{10,1... | collective-permute-start | bytes 3464 | tf_op jit(solution)/shard_map/ppermute | solution.py:21
  129.5 2.1 collective-permute-start.13
  131.6 4.1 %broadcast_in_dim.43 = f32[4,8,4,8,16,8]{5,4,3,2,1,0:T(8,128)} broadcast(f32[4,4,16]{2,1,0:T(4,128)S(1)} %convert_element_type.34), dimensions={0,2,4} | broadcast | bytes 525312 | tf_op jit(solution)/shard_map/broadcast_in_dim | solution.py:31
  135.6 6.4 %reshape.175 = f32[32,32,128]{2,1,0:T(8,128)S(1)} reshape(f32[4,8,4,8,16,8]{5,4,3,2,1,0:T(8,128)} %broadcast_in_dim.43) | data formatting | bytes 1048576 | tf_op jit(solution)/shard_map/reshape | solution.py:34
  142.6 11.6 %broadcast_in_dim.42 = f32[16,2,16,2,64,2]{5,4,3,2,1,0:T(8,128)} broadcast(f32[16,16,64]{2,1,0:T(8,128)S(1)} %fusion.46), dimensions={0,2,4} | broadcast | bytes 589824 | tf_op jit(solution)/shard_map/broadcast_in_dim | solution.py:31
  154.2 24.0 %reshape.174 = f32[32,32,128]{2,1,0:T(8,128)S(1)} reshape(f32[16,2,16,2,64,2]{5,4,3,2,1,0:T(8,128)} %broadcast_in_dim.42) | data formatting | bytes 1048576 | tf_op jit(solution)/shard_map/reshape | solution.py:34
  178.3 1.9 collective-permute-start.14
  180.2 3.4 %collective-permute-start.15 = (f32[1,32,128]{2,1,0:T(8,128)S(1)}, f32[1,32,128]{2,1,0:T(8,128)S(1)}, u32[]{:S(2)}, u32[]{:S(2)}) collective-permute-start(f32[1,32,128]{2,1,0:T(8,128)S(1)} %get-tuple-element.27), channel_id=1, source_target_pairs={{32,0},{64,32},{96,64},{128,96},{160,128},{192,160},{224,192},{33,... | collective-permute-start | bytes 49160 | tf_op jit(solution)/shard_map/ppermute | solution.py:24
  183.6 5.2 %collective-permute-done.15 = f32[1,32,128]{2,1,0:T(8,128)S(1)} collective-permute-done((f32[1,32,128]{2,1,0:T(8,128)S(1)}, f32[1,32,128]{2,1,0:T(8,128)S(1)}, u32[]{:S(2)}, u32[]{:S(2)}) %collective-permute-start.15) | collective-permute-done | bytes 16416 | tf_op jit(solution)/shard_map/ppermute | solution.py:24
  189.5 6.4 %collective-permute-start.16 = (f32[34,32,1]{0,1,2:T(8,128)S(1)}, f32[34,32,1]{0,1,2:T(8,128)S(1)}, u32[]{:S(2)}, u32[]{:S(2)}) collective-permute-start(f32[34,32,1]{0,1,2:T(8,128)S(1)} %copy.59), channel_id=1, source_target_pairs={{0,1},{1,2},{2,3},{3,4},{4,5},{5,6},{6,7},{7,8},{8,9},{9,10},{10,1... | collective-permute-start | bytes 13064 | tf_op jit(solution)/shard_map/ppermute | solution.py:21
  196.3 1.9 collective-permute-start.17
  198.3 4.1 %broadcast_in_dim.44 = f32[4,8,4,8,16,8]{5,4,3,2,1,0:T(8,128)} broadcast(f32[4,4,16]{2,1,0:T(4,128)S(1)} %get-tuple-element.53), dimensions={0,2,4} | broadcast | bytes 525312 | tf_op jit(solution)/shard_map/broadcast_in_dim | solution.py:31
  202.3 6.4 %mul.298 = f32[32,32,128]{2,1,0:T(8,128)S(1)} reshape(f32[4,8,4,8,16,8]{5,4,3,2,1,0:T(8,128)} %broadcast_in_dim.44) | data formatting | bytes 1048576 | tf_op jit(solution)/shard_map/mul | solution.py:62
  208.7 4.1 %broadcast_in_dim.45 = f32[4,8,4,8,16,8]{5,4,3,2,1,0:T(8,128)} broadcast(f32[4,4,16]{2,1,0:T(4,128)S(1)} %get-tuple-element.52), dimensions={0,2,4} | broadcast | bytes 525312 | tf_op jit(solution)/shard_map/broadcast_in_dim | solution.py:31
  212.8 6.4 %reshape.176 = f32[32,32,128]{2,1,0:T(8,128)S(1)} reshape(f32[4,8,4,8,16,8]{5,4,3,2,1,0:T(8,128)} %broadcast_in_dim.45) | data formatting | bytes 1048576 | tf_op jit(solution)/shard_map/reshape | solution.py:34
  221.1 1.7 select_maximum_fusion.8
  224.0 1.9 collective-permute-start.18
  226.0 3.4 %collective-permute-start.19 = (f32[1,32,128]{2,1,0:T(8,128)S(1)}, f32[1,32,128]{2,1,0:T(8,128)S(1)}, u32[]{:S(2)}, u32[]{:S(2)}) collective-permute-start(f32[1,32,128]{2,1,0:T(8,128)S(1)} %get-tuple-element.25), channel_id=1, source_target_pairs={{32,0},{64,32},{96,64},{128,96},{160,128},{192,160},{224,192},{33,... | collective-permute-start | bytes 49160 | tf_op jit(solution)/shard_map/ppermute | solution.py:24
  229.4 4.7 %collective-permute-done.19 = f32[1,32,128]{2,1,0:T(8,128)S(1)} collective-permute-done((f32[1,32,128]{2,1,0:T(8,128)S(1)}, f32[1,32,128]{2,1,0:T(8,128)S(1)}, u32[]{:S(2)}, u32[]{:S(2)}) %collective-permute-start.19) | collective-permute-done | bytes 16416 | tf_op jit(solution)/shard_map/ppermute | solution.py:24
  236.6 7.1 %collective-permute-start.20 = (f32[34,32,1]{0,1,2:T(8,128)S(1)}, f32[34,32,1]{0,1,2:T(8,128)S(1)}, u32[]{:S(2)}, u32[]{:S(2)}) collective-permute-start(f32[34,32,1]{0,1,2:T(8,128)S(1)} %copy.63), channel_id=1, source_target_pairs={{0,1},{1,2},{2,3},{3,4},{4,5},{5,6},{6,7},{7,8},{8,9},{9,10},{10,1... | collective-permute-start | bytes 13064 | tf_op jit(solution)/shard_map/ppermute | solution.py:21
  244.1 1.9 collective-permute-start.21
  246.6 4.6 %collective-permute-done.21 = f32[34,32,1]{0,1,2:T(8,128)S(1)} collective-permute-done((f32[34,32,1]{0,1,2:T(8,128)S(1)}, f32[34,32,1]{0,1,2:T(8,128)S(1)}, u32[]{:S(2)}, u32[]{:S(2)}) %collective-permute-start.21) | collective-permute-done | bytes 4384 | tf_op jit(solution)/shard_map/ppermute | solution.py:24
  255.5 1.9 collective-permute-start.22
  257.4 3.4 %collective-permute-start.23 = (f32[1,32,128]{2,1,0:T(8,128)S(1)}, f32[1,32,128]{2,1,0:T(8,128)S(1)}, u32[]{:S(2)}, u32[]{:S(2)}) collective-permute-start(f32[1,32,128]{2,1,0:T(8,128)S(1)} %get-tuple-element.23), channel_id=1, source_target_pairs={{32,0},{64,32},{96,64},{128,96},{160,128},{192,160},{224,192},{33,... | collective-permute-start | bytes 49160 | tf_op jit(solution)/shard_map/ppermute | solution.py:24
  260.8 4.7 %collective-permute-done.23 = f32[1,32,128]{2,1,0:T(8,128)S(1)} collective-permute-done((f32[1,32,128]{2,1,0:T(8,128)S(1)}, f32[1,32,128]{2,1,0:T(8,128)S(1)}, u32[]{:S(2)}, u32[]{:S(2)}) %collective-permute-start.23) | collective-permute-done | bytes 16416 | tf_op jit(solution)/shard_map/ppermute | solution.py:24
  268.0 3.1 %collective-permute-start.24 = (f32[34,32,1]{0,1,2:T(8,128)S(1)}, f32[34,32,1]{0,1,2:T(8,128)S(1)}, u32[]{:S(2)}, u32[]{:S(2)}) collective-permute-start(f32[34,32,1]{0,1,2:T(8,128)S(1)} %copy.67), channel_id=1, source_target_pairs={{0,1},{1,2},{2,3},{3,4},{4,5},{5,6},{6,7},{7,8},{8,9},{9,10},{10,1... | collective-permute-start | bytes 13064 | tf_op jit(solution)/shard_map/ppermute | solution.py:21
  271.5 1.9 collective-permute-start.25
  274.1 4.6 %collective-permute-done.25 = f32[34,32,1]{0,1,2:T(8,128)S(1)} collective-permute-done((f32[34,32,1]{0,1,2:T(8,128)S(1)}, f32[34,32,1]{0,1,2:T(8,128)S(1)}, u32[]{:S(2)}, u32[]{:S(2)}) %collective-permute-start.25) | collective-permute-done | bytes 4384 | tf_op jit(solution)/shard_map/ppermute | solution.py:24
  (110 shorter events, 32.8 us)
Async XLA Ops:
  0.6 10.0 %collective-permute-start = (f32[1,4,512]{2,1,0:T(4,128)}, f32[1,4,512]{2,1,0:T(4,128)S(1)}, u32[]{:S(2)}, u32[]{:S(2)}) collective-permute-start(f32[1,4,512]{2,1,0:T(4,128)} %param.11), channel_id=1, source_target_pairs={{0,1},{1,2},{2,3},{3,4},{4,5},{5,6},{6,7},{7,8},{8,9},{9,10},{10,1... | collective-permute-start | bytes 24584 | tf_op jit(solution)/shard_map/ppermute | solution.py:21
  5.8 7.3 %collective-permute-start.1 = (f32[1,4,512]{2,1,0:T(4,128)}, f32[1,4,512]{2,1,0:T(4,128)S(1)}, u32[]{:S(2)}, u32[]{:S(2)}) collective-permute-start(f32[1,4,512]{2,1,0:T(4,128)} %param.11), channel_id=1, source_target_pairs={{1,0},{2,1},{3,2},{4,3},{5,4},{6,5},{7,6},{8,7},{9,8},{10,9},{11,1... | collective-permute-start | bytes 24584 | tf_op jit(solution)/shard_map/ppermute | solution.py:24
  9.5 3.6 %copy-start.3 = (f32[1,4,512]{2,1,0:T(4,128)S(1)}, f32[1,4,512]{2,1,0:T(4,128)}, u32[]{:S(2)}) copy-start(f32[1,4,512]{2,1,0:T(4,128)} %param.11) | copy-start | bytes 24580
  16.7 6.8 %copy-start.4 = (s32[4,4,16]{2,1,0:T(4,128)S(1)}, s32[4,4,16]{2,1,0:T(4,128)}, u32[]{:S(2)}) copy-start(s32[4,4,16]{2,1,0:T(4,128)} %param.8) | copy-start | bytes 3076
  16.7 6.8 %copy-start.5 = (f32[16]{0:T(128)S(1)}, f32[16]{0:T(128)}, u32[]{:S(2)}) copy-start(f32[16]{0:T(128)} %param.9) | copy-start | bytes 196
  17.1 19.9 %copy-start.2 = (s32[4,4,16]{2,1,0:T(4,128)S(1)}, s32[4,4,16]{2,1,0:T(4,128)}, u32[]{:S(2)}) copy-start(s32[4,4,16]{2,1,0:T(4,128)} %param.7) | copy-start | bytes 3076
  17.4 6.3 %collective-permute-start.2 = (f32[1,16,64]{2,1,0:T(8,128)S(1)}, f32[1,16,64]{2,1,0:T(8,128)S(1)}, u32[]{:S(2)}, u32[]{:S(2)}) collective-permute-start(f32[1,16,64]{2,1,0:T(8,128)S(1)} %get-tuple-element.50), channel_id=1, source_target_pairs={{0,32},{32,64},{64,96},{96,128},{128,160},{160,192},{192,224},{1,3... | collective-permute-start | bytes 12296 | tf_op jit(solution)/shard_map/ppermute | solution.py:21
  21.6 8.1 %collective-permute-start.3 = (f32[1,16,64]{2,1,0:T(8,128)S(1)}, f32[1,16,64]{2,1,0:T(8,128)S(1)}, u32[]{:S(2)}, u32[]{:S(2)}) collective-permute-start(f32[1,16,64]{2,1,0:T(8,128)S(1)} %get-tuple-element.51), channel_id=1, source_target_pairs={{32,0},{64,32},{96,64},{128,96},{160,128},{192,160},{224,192},{33,... | collective-permute-start | bytes 12296 | tf_op jit(solution)/shard_map/ppermute | solution.py:24
  29.8 59.9 %collective-permute-start.4 = (f32[18,16,1]{2,1,0:T(8,128)S(1)}, f32[18,16,1]{2,1,0:T(8,128)S(1)}, u32[]{:S(2)}, u32[]{:S(2)}) collective-permute-start(f32[18,16,1]{2,1,0:T(8,128)S(1)} %get-tuple-element.44), channel_id=1, source_target_pairs={{0,1},{1,2},{2,3},{3,4},{4,5},{5,6},{6,7},{7,8},{8,9},{9,10},{10,1... | collective-permute-start | bytes 3464 | tf_op jit(solution)/shard_map/ppermute | solution.py:21
  35.0 54.6 %collective-permute-start.5 = (f32[18,16,1]{2,1,0:T(8,128)S(1)}, f32[18,16,1]{2,1,0:T(8,128)S(1)}, u32[]{:S(2)}, u32[]{:S(2)}) collective-permute-start(f32[18,16,1]{2,1,0:T(8,128)S(1)} %get-tuple-element.45), channel_id=1, source_target_pairs={{1,0},{2,1},{3,2},{4,3},{5,4},{6,5},{7,6},{8,7},{9,8},{10,9},{11,1... | collective-permute-start | bytes 3464 | tf_op jit(solution)/shard_map/ppermute | solution.py:24
  39.8 2.7 copy-start
  90.3 5.3 %collective-permute-start.6 = (f32[1,16,64]{2,1,0:T(8,128)S(1)}, f32[1,16,64]{2,1,0:T(8,128)S(1)}, u32[]{:S(2)}, u32[]{:S(2)}) collective-permute-start(f32[1,16,64]{2,1,0:T(8,128)S(1)} %get-tuple-element.48), channel_id=1, source_target_pairs={{0,32},{32,64},{64,96},{96,128},{128,160},{160,192},{192,224},{1,3... | collective-permute-start | bytes 12296 | tf_op jit(solution)/shard_map/ppermute | solution.py:21
  92.2 8.0 %collective-permute-start.7 = (f32[1,16,64]{2,1,0:T(8,128)S(1)}, f32[1,16,64]{2,1,0:T(8,128)S(1)}, u32[]{:S(2)}, u32[]{:S(2)}) collective-permute-start(f32[1,16,64]{2,1,0:T(8,128)S(1)} %get-tuple-element.49), channel_id=1, source_target_pairs={{32,0},{64,32},{96,64},{128,96},{160,128},{192,160},{224,192},{33,... | collective-permute-start | bytes 12296 | tf_op jit(solution)/shard_map/ppermute | solution.py:24
  100.3 9.1 %collective-permute-start.8 = (f32[18,16,1]{2,1,0:T(8,128)S(1)}, f32[18,16,1]{2,1,0:T(8,128)S(1)}, u32[]{:S(2)}, u32[]{:S(2)}) collective-permute-start(f32[18,16,1]{2,1,0:T(8,128)S(1)} %get-tuple-element.42), channel_id=1, source_target_pairs={{0,1},{1,2},{2,3},{3,4},{4,5},{5,6},{6,7},{7,8},{8,9},{9,10},{10,1... | collective-permute-start | bytes 3464 | tf_op jit(solution)/shard_map/ppermute | solution.py:21
  107.3 8.6 %collective-permute-start.9 = (f32[18,16,1]{2,1,0:T(8,128)S(1)}, f32[18,16,1]{2,1,0:T(8,128)S(1)}, u32[]{:S(2)}, u32[]{:S(2)}) collective-permute-start(f32[18,16,1]{2,1,0:T(8,128)S(1)} %get-tuple-element.43), channel_id=1, source_target_pairs={{1,0},{2,1},{3,2},{4,3},{5,4},{6,5},{7,6},{8,7},{9,8},{10,9},{11,1... | collective-permute-start | bytes 3464 | tf_op jit(solution)/shard_map/ppermute | solution.py:24
  116.5 5.3 %collective-permute-start.10 = (f32[1,16,64]{2,1,0:T(8,128)S(1)}, f32[1,16,64]{2,1,0:T(8,128)S(1)}, u32[]{:S(2)}, u32[]{:S(2)}) collective-permute-start(f32[1,16,64]{2,1,0:T(8,128)S(1)} %get-tuple-element.46), channel_id=1, source_target_pairs={{0,32},{32,64},{64,96},{96,128},{128,160},{160,192},{192,224},{1,3... | collective-permute-start | bytes 12296 | tf_op jit(solution)/shard_map/ppermute | solution.py:21
  118.4 8.0 %collective-permute-start.11 = (f32[1,16,64]{2,1,0:T(8,128)S(1)}, f32[1,16,64]{2,1,0:T(8,128)S(1)}, u32[]{:S(2)}, u32[]{:S(2)}) collective-permute-start(f32[1,16,64]{2,1,0:T(8,128)S(1)} %get-tuple-element.47), channel_id=1, source_target_pairs={{32,0},{64,32},{96,64},{128,96},{160,128},{192,160},{224,192},{33,... | collective-permute-start | bytes 12296 | tf_op jit(solution)/shard_map/ppermute | solution.py:24
  126.5 15.5 %collective-permute-start.12 = (f32[18,16,1]{2,1,0:T(8,128)S(1)}, f32[18,16,1]{2,1,0:T(8,128)S(1)}, u32[]{:S(2)}, u32[]{:S(2)}) collective-permute-start(f32[18,16,1]{2,1,0:T(8,128)S(1)} %get-tuple-element.40), channel_id=1, source_target_pairs={{0,1},{1,2},{2,3},{3,4},{4,5},{5,6},{6,7},{7,8},{8,9},{9,10},{10,1... | collective-permute-start | bytes 3464 | tf_op jit(solution)/shard_map/ppermute | solution.py:21
  129.5 12.6 %collective-permute-start.13 = (f32[18,16,1]{2,1,0:T(8,128)S(1)}, f32[18,16,1]{2,1,0:T(8,128)S(1)}, u32[]{:S(2)}, u32[]{:S(2)}) collective-permute-start(f32[18,16,1]{2,1,0:T(8,128)S(1)} %get-tuple-element.41), channel_id=1, source_target_pairs={{1,0},{2,1},{3,2},{4,3},{5,4},{6,5},{7,6},{8,7},{9,8},{10,9},{11,1... | collective-permute-start | bytes 3464 | tf_op jit(solution)/shard_map/ppermute | solution.py:24
  142.6 11.6 %copy-start.1 = (f32[16,16,64]{2,1,0:T(8,128)}, f32[16,16,64]{2,1,0:T(8,128)S(1)}, u32[]{:S(2)}) copy-start(f32[16,16,64]{2,1,0:T(8,128)S(1)} %fusion.46) | copy-start | bytes 196612
  178.3 5.3 %collective-permute-start.14 = (f32[1,32,128]{2,1,0:T(8,128)S(1)}, f32[1,32,128]{2,1,0:T(8,128)S(1)}, u32[]{:S(2)}, u32[]{:S(2)}) collective-permute-start(f32[1,32,128]{2,1,0:T(8,128)S(1)} %get-tuple-element.26), channel_id=1, source_target_pairs={{0,32},{32,64},{64,96},{96,128},{128,160},{160,192},{192,224},{1,3... | collective-permute-start | bytes 49160 | tf_op jit(solution)/shard_map/ppermute | solution.py:21
  180.2 8.5 %collective-permute-start.15 = (f32[1,32,128]{2,1,0:T(8,128)S(1)}, f32[1,32,128]{2,1,0:T(8,128)S(1)}, u32[]{:S(2)}, u32[]{:S(2)}) collective-permute-start(f32[1,32,128]{2,1,0:T(8,128)S(1)} %get-tuple-element.27), channel_id=1, source_target_pairs={{32,0},{64,32},{96,64},{128,96},{160,128},{192,160},{224,192},{33,... | collective-permute-start | bytes 49160 | tf_op jit(solution)/shard_map/ppermute | solution.py:24
  189.5 29.7 %collective-permute-start.16 = (f32[34,32,1]{0,1,2:T(8,128)S(1)}, f32[34,32,1]{0,1,2:T(8,128)S(1)}, u32[]{:S(2)}, u32[]{:S(2)}) collective-permute-start(f32[34,32,1]{0,1,2:T(8,128)S(1)} %copy.59), channel_id=1, source_target_pairs={{0,1},{1,2},{2,3},{3,4},{4,5},{5,6},{6,7},{7,8},{8,9},{9,10},{10,1... | collective-permute-start | bytes 13064 | tf_op jit(solution)/shard_map/ppermute | solution.py:21
  196.3 23.4 %collective-permute-start.17 = (f32[34,32,1]{0,1,2:T(8,128)S(1)}, f32[34,32,1]{0,1,2:T(8,128)S(1)}, u32[]{:S(2)}, u32[]{:S(2)}) collective-permute-start(f32[34,32,1]{0,1,2:T(8,128)S(1)} %copy.60), channel_id=1, source_target_pairs={{1,0},{2,1},{3,2},{4,3},{5,4},{6,5},{7,6},{8,7},{9,8},{10,9},{11,1... | collective-permute-start | bytes 13064 | tf_op jit(solution)/shard_map/ppermute | solution.py:24
  224.0 5.3 %collective-permute-start.18 = (f32[1,32,128]{2,1,0:T(8,128)S(1)}, f32[1,32,128]{2,1,0:T(8,128)S(1)}, u32[]{:S(2)}, u32[]{:S(2)}) collective-permute-start(f32[1,32,128]{2,1,0:T(8,128)S(1)} %get-tuple-element.24), channel_id=1, source_target_pairs={{0,32},{32,64},{64,96},{96,128},{128,160},{160,192},{192,224},{1,3... | collective-permute-start | bytes 49160 | tf_op jit(solution)/shard_map/ppermute | solution.py:21
  226.0 8.1 %collective-permute-start.19 = (f32[1,32,128]{2,1,0:T(8,128)S(1)}, f32[1,32,128]{2,1,0:T(8,128)S(1)}, u32[]{:S(2)}, u32[]{:S(2)}) collective-permute-start(f32[1,32,128]{2,1,0:T(8,128)S(1)} %get-tuple-element.25), channel_id=1, source_target_pairs={{32,0},{64,32},{96,64},{128,96},{160,128},{192,160},{224,192},{33,... | collective-permute-start | bytes 49160 | tf_op jit(solution)/shard_map/ppermute | solution.py:24
  236.6 9.5 %collective-permute-start.20 = (f32[34,32,1]{0,1,2:T(8,128)S(1)}, f32[34,32,1]{0,1,2:T(8,128)S(1)}, u32[]{:S(2)}, u32[]{:S(2)}) collective-permute-start(f32[34,32,1]{0,1,2:T(8,128)S(1)} %copy.63), channel_id=1, source_target_pairs={{0,1},{1,2},{2,3},{3,4},{4,5},{5,6},{6,7},{7,8},{8,9},{9,10},{10,1... | collective-permute-start | bytes 13064 | tf_op jit(solution)/shard_map/ppermute | solution.py:21
  244.1 7.2 %collective-permute-start.21 = (f32[34,32,1]{0,1,2:T(8,128)S(1)}, f32[34,32,1]{0,1,2:T(8,128)S(1)}, u32[]{:S(2)}, u32[]{:S(2)}) collective-permute-start(f32[34,32,1]{0,1,2:T(8,128)S(1)} %copy.64), channel_id=1, source_target_pairs={{1,0},{2,1},{3,2},{4,3},{5,4},{6,5},{7,6},{8,7},{9,8},{10,9},{11,1... | collective-permute-start | bytes 13064 | tf_op jit(solution)/shard_map/ppermute | solution.py:24
  255.5 5.3 %collective-permute-start.22 = (f32[1,32,128]{2,1,0:T(8,128)S(1)}, f32[1,32,128]{2,1,0:T(8,128)S(1)}, u32[]{:S(2)}, u32[]{:S(2)}) collective-permute-start(f32[1,32,128]{2,1,0:T(8,128)S(1)} %get-tuple-element.22), channel_id=1, source_target_pairs={{0,32},{32,64},{64,96},{96,128},{128,160},{160,192},{192,224},{1,3... | collective-permute-start | bytes 49160 | tf_op jit(solution)/shard_map/ppermute | solution.py:21
  257.4 8.1 %collective-permute-start.23 = (f32[1,32,128]{2,1,0:T(8,128)S(1)}, f32[1,32,128]{2,1,0:T(8,128)S(1)}, u32[]{:S(2)}, u32[]{:S(2)}) collective-permute-start(f32[1,32,128]{2,1,0:T(8,128)S(1)} %get-tuple-element.23), channel_id=1, source_target_pairs={{32,0},{64,32},{96,64},{128,96},{160,128},{192,160},{224,192},{33,... | collective-permute-start | bytes 49160 | tf_op jit(solution)/shard_map/ppermute | solution.py:24
  268.0 5.4 %collective-permute-start.24 = (f32[34,32,1]{0,1,2:T(8,128)S(1)}, f32[34,32,1]{0,1,2:T(8,128)S(1)}, u32[]{:S(2)}, u32[]{:S(2)}) collective-permute-start(f32[34,32,1]{0,1,2:T(8,128)S(1)} %copy.67), channel_id=1, source_target_pairs={{0,1},{1,2},{2,3},{3,4},{4,5},{5,6},{6,7},{7,8},{8,9},{9,10},{10,1... | collective-permute-start | bytes 13064 | tf_op jit(solution)/shard_map/ppermute | solution.py:21
  271.5 7.2 %collective-permute-start.25 = (f32[34,32,1]{0,1,2:T(8,128)S(1)}, f32[34,32,1]{0,1,2:T(8,128)S(1)}, u32[]{:S(2)}, u32[]{:S(2)}) collective-permute-start(f32[34,32,1]{0,1,2:T(8,128)S(1)} %copy.68), channel_id=1, source_target_pairs={{1,0},{2,1},{3,2},{4,3},{5,4},{6,5},{7,6},{8,7},{9,8},{10,9},{11,1... | collective-permute-start | bytes 13064 | tf_op jit(solution)/shard_map/ppermute | solution.py:24
where the time goes:
time: 285 us; the launch traced here: 284 us
  local copies, waits for them, and re-layouts  124 us (44%)
  starting transfers between devices  83 us (29%)
  waiting for transfers between devices  48.2 us (17%)
  other arithmetic  26.8 us (9%)
    ppermute x13, starting transfers between devices, extended(): lax.ppermute(lax.slice_in_dim(block, block.shape[dim] - width, None, axis...  50.7 us
    ppermute x13, waiting for transfers between devices, extended(): lax.ppermute(lax.slice_in_dim(block, 0, width, axis=dim), axis, backward)  48.1 us
    reshape x5, local copies, waits for them, and re-layouts, expand(): return wide.reshape(first * factor, second * factor, third * factor)  40.5 us
    reshape x1, local copies, waits for them, and re-layouts, local(): source.reshape(size_x // 2, 2, size_y // 2, 2, size_z // 2, 2)  34.9 us
    ppermute x13, starting transfers between devices, extended(): lax.ppermute(lax.slice_in_dim(block, 0, width, axis=dim), axis, backward)  32.3 us
    broadcast_in_dim x7, local copies, waits for them, and re-layouts, expand(): jnp.broadcast_to(values[:, None, :, None, :, None], (first, factor, secon...  25.8 us
    reduce_sum x1, other arithmetic, local(): source.reshape(size_x // 2, 2, size_y // 2, 2, size_z // 2, 2)  12.2 us
    mul x2, local copies, waits for them, and re-layouts, relax_step(): relaxation * inverse * (source - laplace - screen * mass_all)  7.4 us
  transfers between devices with their start and end apart: 26, of which 11 were waited for; matrix products, arithmetic and copies ran while one was open for 32% of the time, Pallas kernels for 0%

commit v1 on v0

v1 whole, which is shorter than its diff:
```python
import jax
import jax.numpy as jnp
from jax import lax
from jax.experimental import pallas as pl
from jax.experimental.pallas import tpu as pltpu
from jax.sharding import PartitionSpec as P

BRICK = 8
SWEEPS = 3

screen_strength = 4.0
relaxation = 2.0 / 3.0
stiff_diagonal = 8.0 / 3.0
mass_diagonal = 8.0 / 27.0

F32 = jnp.float32
HI = lax.Precision.HIGHEST
VMEM = pltpu.VMEM
SMEM = pltpu.SMEM

CX, NY, CZ = 32, 32, 128
LANES = 128
COARSE = 4
UNROLL = 8

Z_COARSE, Z_POS, Z_BRICK, Z_SRC, Z_ROWS = 0, 16, 24, 56, 120
X_START, X_MID, X_FINE, X_GHOST, X_BRICK, X_ROWS = 0, 48, 112, 176, 184, 200


def iota(shape, dim):
    return lax.broadcasted_iota(jnp.int32, shape, dim)


def onehot(mask):
    return jnp.where(mask, 1.0, 0.0).astype(F32)


def dot(a, b):
    return jnp.dot(a, b, precision=HI, preferred_element_type=F32)


def turn(v, shift):
    shift = shift % LANES
    return v if shift == 0 else pltpu.roll(v, shift, v.ndim - 1)


def pack_z(src, occ, cls, tab, par, co, zl, zr, pown):
    first = (lax.axis_index("slab") - 1) * COARSE
    for t in range(4):
        part = co[0, :, LANES * t : LANES * (t + 1)]
        zl[Z_COARSE + 4 * t : Z_COARSE + 4 * t + 4, :] = part
        zr[Z_COARSE + 4 * t : Z_COARSE + 4 * t + 4, :] = part
    zl[Z_POS : Z_POS + 8, :] = jnp.full((8, LANES), par[0, 0, 0] - first, jnp.int32).astype(F32)
    zr[Z_POS : Z_POS + 8, :] = jnp.full((8, LANES), par[0, 0, 7] - first, jnp.int32).astype(F32)
    pown[...] = jnp.zeros((32, LANES), F32)
    for bx in range(4):
        occupied = occ[bx].astype(F32)
        labels = cls[bx]
        weight = jnp.zeros((4, 16), F32)
        for c in range(16):
            weight = weight + jnp.where(labels == c, tab[c], 0.0)
        screen = screen_strength * weight
        pown[4 * bx : 4 * bx + 4, 0:16] = occupied / (stiff_diagonal + screen * mass_diagonal)
        pown[16 + 4 * bx : 20 + 4 * bx, 0:16] = screen
    bricks = pown[...]
    lane = iota((32, LANES), 1)
    zl[Z_BRICK : Z_BRICK + 32, :] = jnp.where((lane == 16) | (lane == 17), turn(bricks, 16), 0.0)
    zr[Z_BRICK : Z_BRICK + 32, :] = jnp.where(lane >= 126, turn(bricks, 112), 0.0)
    slot = iota((NY, LANES), 1) // 8
    for g in range(2):
        left = jnp.zeros((NY, LANES), F32)
        right = jnp.zeros((NY, LANES), F32)
        for i in range(16):
            v = src[16 * g + i]
            left = jnp.where(slot == i, turn(v, 8 * i), left)
            right = jnp.where(slot == i, turn(v, 8 * i + 8), right)
        zl[Z_SRC + NY * g : Z_SRC + NY * (g + 1), :] = left
        zr[Z_SRC + NY * g : Z_SRC + NY * (g + 1), :] = right


def extend_z(src, par, co, pown, hl, hr, fl, fr, xl, xr, start, mid, ghost, bricks, cand, pairs):
    first = (lax.axis_index("slab") - 2) * COARSE
    cand[20:24, :] = jnp.zeros((4, 512), F32)
    cand[0:4, :] = fl[0]
    cand[8:12, :] = co[0]
    cand[16:20, :] = fr[0]
    for t in range(4):
        cand[4:8, LANES * t : LANES * (t + 1)] = hl[Z_COARSE + 4 * t : Z_COARSE + 4 * t + 4, :]
        cand[12:16, LANES * t : LANES * (t + 1)] = hr[Z_COARSE + 4 * t : Z_COARSE + 4 * t + 4, :]
    sub, lane = iota((8, LANES), 0), iota((8, LANES), 1)
    chosen = jnp.full((8, LANES), -1, jnp.int32)
    for k in range(4):
        chosen = jnp.where(sub == k + 1, par[0, 0, 2 * k] - first, chosen)
    chosen = chosen.astype(F32)
    chosen = jnp.where(sub == 0, hl[Z_POS : Z_POS + 8, :], chosen)
    chosen = jnp.where(sub == 5, hr[Z_POS : Z_POS + 8, :] + 2.0 * COARSE, chosen)
    pick = onehot(chosen == lane.astype(F32))
    six = dot(pick[:, 0:24], cand[...])
    row2, lane2 = iota((32, LANES), 0), iota((32, LANES), 1)
    spread = onehot(lane2 // 8 == (row2 // 16) * 8 + row2 % 16 // 2)
    c, z = iota((LANES, LANES), 0), iota((LANES, LANES), 1)
    place = onehot(c % 8 == z % 16 // 2)
    zone = iota((32, LANES), 1) // 16
    for t in range(4):
        rows = jnp.concatenate(
            [
                jnp.broadcast_to(six[k : k + 1, LANES * t : LANES * (t + 1)], (32, LANES)) * spread
                for k in range(6)
            ],
            axis=0,
        )
        placed = dot(rows, place)
        total = jnp.zeros((32, LANES), F32)
        for k in range(6):
            total = jnp.where(zone == (7 if k == 0 else k - 1), placed[32 * k : 32 * (k + 1)], total)
        start[32 * t : 32 * (t + 1), :] = total
    bricks[...] = pown[...] + hl[Z_BRICK : Z_BRICK + 32, :] + hr[Z_BRICK : Z_BRICK + 32, :]
    lane32 = iota((NY, LANES), 1)
    for g in range(2):
        left = hl[Z_SRC + NY * g : Z_SRC + NY * (g + 1), :]
        right = hr[Z_SRC + NY * g : Z_SRC + NY * (g + 1), :]
        for i in range(16):
            ghost[16 * g + i] = jnp.where(
                lane32 < 8, turn(right, -8 * i), jnp.where(lane32 >= 120, turn(left, -8 * i - 8), 0.0)
            )
    z2, l2 = iota((2 * LANES, LANES), 0), iota((2 * LANES, LANES), 1)
    join = (z2 < 128) & (z2 // 2 == l2)
    join = join | ((z2 >= 128) & (z2 < 136) & (l2 == 64 + (z2 - 128) // 2))
    join = join | ((z2 >= 248) & (l2 == z2 // 2))
    join = onehot(join)
    for i in range(16):
        for part, ref in ((0, src), (1, ghost)):
            a = ref[2 * i, pl.ds(0, 16, 2), :] + ref[2 * i, pl.ds(1, 16, 2), :]
            b = ref[2 * i + 1, pl.ds(0, 16, 2), :] + ref[2 * i + 1, pl.ds(1, 16, 2), :]
            pairs[16 * i : 16 * (i + 1), LANES * part : LANES * (part + 1)] = a + b
    summed = 0.25 * dot(pairs[...], join)
    for i in range(16):
        mid[i] = summed[16 * i : 16 * (i + 1)]
    for out, rows, m0, f0, b0 in ((xl, 0, 0, 0, 0), (xr, 80, 12, 30, 2)):
        out[X_START : X_START + 48, :] = start[rows : rows + 48, :]
        packed = jnp.zeros((8, LANES), F32)
        for i in range(4):
            out[X_MID + 16 * i : X_MID + 16 * (i + 1), :] = mid[m0 + i]
        for i in range(2):
            out[X_FINE + NY * i : X_FINE + NY * (i + 1), :] = src[f0 + i]
            edge = ghost[f0 + i]
            for y in range(4):
                slot = 4 * i + y
                moved = turn(edge[8 * y : 8 * y + 8], 16 * slot + 8)
                packed = jnp.where(lane // 16 == slot, moved, packed)
        out[X_GHOST : X_GHOST + 8, :] = packed
        out[X_BRICK : X_BRICK + 8, :] = bricks[4 * b0 : 4 * b0 + 8, :]
        out[X_BRICK + 8 : X_BRICK + 16, :] = bricks[16 + 4 * b0 : 24 + 4 * b0, :]


def up_down(v):
    rows = v.shape[0]
    y = iota(v.shape, 0)
    up = jnp.where(y == 0, 0.0, pltpu.roll(v, 1, 0))
    down = jnp.where(y == rows - 1, 0.0, pltpu.roll(v, rows - 1, 0))
    return up + down


def along_y(v, z_sum):
    a = 4.0 * v + z_sum
    b = 4.0 * v + up_down(v)
    c = 4.0 * a + up_down(a)
    return a + b, c


def relax(v, rhs, inverse, weight, before, here, after):
    d = 4.0 * here[0] + (before[0] + after[0])
    e = 4.0 * here[1] + (before[1] + after[1])
    return v + inverse * (rhs - (here[1] + d) * (1.0 / 6.0) - weight * e)


def sweep_all(
    src, xl, xr, start, smid, sghost, bricks, mid_out, fin_out,
    v13, pext, i13, w13, i14, w14, i14g, w14g, m0, g0, m1, g1, fine, fghost,
):
    pext[0:8, :] = xl[X_BRICK : X_BRICK + 8, :]
    pext[8:24, :] = bricks[0:16, :]
    pext[24:32, :] = xr[X_BRICK : X_BRICK + 8, :]
    pext[32:40, :] = xl[X_BRICK + 8 : X_BRICK + 16, :]
    pext[40:56, :] = bricks[16:32, :]
    pext[56:64, :] = xr[X_BRICK + 8 : X_BRICK + 16, :]
    b, l = iota((LANES, 3 * LANES), 0), iota((LANES, 3 * LANES), 1)
    ring = l % LANES
    hit = (l < 128) & (b == jnp.where(ring >= 96, ring // 4 + 96, ring // 4))
    hit = hit | ((l >= 128) & (l < 256) & (b == ring // 8))
    hit = hit | ((l >= 256) & (b == jnp.where(ring >= 64, ring // 8 + 112, ring // 8 + 16)))
    spread = dot(pext[...], onehot(hit))
    factor = relaxation * spread[0:32]
    weight = spread[32:64] * (1.0 / 216.0) - (1.0 / 12.0)
    half = iota((8, LANES), 0) < 4
    for bx in range(8):
        for t in range(2):
            r = 4 * bx + 2 * t
            for table, out in ((factor, i13), (weight, w13)):
                upper = jnp.broadcast_to(table[r : r + 1, 0:LANES], (8, LANES))
                lower = jnp.broadcast_to(table[r + 1 : r + 2, 0:LANES], (8, LANES))
                out[bx, 8 * t : 8 * t + 8, :] = jnp.where(half, upper, lower)
    for bx in range(1, 7):
        for by in range(4):
            r = 4 * bx + by
            for table, out, col in ((factor, i14, 1), (weight, w14, 1), (factor, i14g, 2), (weight, w14g, 2)):
                row = table[r : r + 1, LANES * col : LANES * (col + 1)]
                out[bx - 1, 8 * by : 8 * by + 8, :] = jnp.broadcast_to(row, (8, LANES))

    for x in range(-5, 21):
        q = x // 2
        if q < 0:
            v = xr_rows(xl, X_START + 16 * (q + 3))
        elif q > 7:
            v = xr_rows(xr, X_START + 16 * (q - 8))
        else:
            v = start[16 * q : 16 * (q + 1), :]
        v13[x + 5] = jnp.where(i13[x // 4 + 2] != 0.0, v, 0.0)

    def rhs13(x):
        if x < 0:
            return xl[X_MID + 16 * (x + 4) : X_MID + 16 * (x + 5), :]
        if x > 15:
            return xr[X_MID + 16 * (x - 16) : X_MID + 16 * (x - 15), :]
        return smid[x]

    for n in range(SWEEPS):
        low, high = -4 + n, 19 - n
        planes = {}
        for x in range(low - 1, high + 2):
            v = v13[x + 5]
            planes[x] = along_y(v, turn(v, 1) + turn(v, -1))
            if x > low:
                o = x - 1
                bx = o // 4 + 2
                v13[o + 5] = relax(
                    v13[o + 5], rhs13(o), i13[bx], w13[bx], planes[o - 1], planes[o], planes[o + 1]
                )
    for x in range(16):
        mid_out[x] = v13[x + 5, :, 0:64]

    b, l = iota((LANES, 2 * LANES), 0), iota((LANES, 2 * LANES), 1)
    lift = ((l < 128) & (b == l // 2)) | ((l >= 128) & (l < 192) & (b == l // 2)) | ((l >= 192) & (b == l // 2))
    lift = onehot(lift)
    parents = jnp.concatenate(
        [jnp.where(i13[x // 4 + 2] != 0.0, v13[x + 5], 0.0) for x in range(-2, 18)], axis=0
    )
    lifted = dot(parents, lift)
    for x in range(-2, 18):
        rows = lifted[16 * (x + 2) : 16 * (x + 3)]
        for child in (2 * x, 2 * x + 1):
            if -3 <= child <= 34:
                for parity in range(2):
                    m0[child + 3, pl.ds(parity, 16, 2), :] = rows[:, 0:LANES]
                    g0[child + 3, pl.ds(parity, 16, 2), :] = rows[:, LANES:]
    lane8 = iota((8, LANES), 1)
    valid = (lane8 < 8) | (lane8 >= 120)
    for i in range(2):
        fine[i] = xl[X_FINE + NY * i : X_FINE + NY * (i + 1), :]
        fine[34 + i] = xr[X_FINE + NY * i : X_FINE + NY * (i + 1), :]
        for y in range(4):
            slot = 4 * i + y
            for edge, at in ((xl, i), (xr, 34 + i)):
                moved = turn(edge[X_GHOST : X_GHOST + 8, :], -(16 * slot + 8))
                fghost[at, 8 * y : 8 * y + 8, :] = jnp.where(valid, moved, 0.0)

    lane = iota((NY, LANES), 1)

    def sums(vm, vg, want_main):
        mr, gr, ml, gl = turn(vm, 1), turn(vg, 1), turn(vm, -1), turn(vg, -1)
        if want_main:
            return jnp.where(lane == 0, gr, mr) + jnp.where(lane == 127, gl, ml)
        return jnp.where(lane == 0, mr, gr) + jnp.where(lane == 127, ml, gl)

    def rhs14(x, main):
        if isinstance(x, int) and (x < 0 or x > 31):
            return (fine if main else fghost)[x + 2 if x < 0 else x + 2]
        return (src if main else sghost)[x]

    def sweep14(n, main, vm, vg, out, last):
        low, high = -2 + n, 33 - n
        inv, wgt = (i14, w14) if main else (i14g, w14g)
        own = vm if main else vg

        def plane(x):
            a, g = vm[x + 3], vg[x + 3]
            return along_y(a if main else g, sums(a, g, main))

        def write(x, bx, before, here, after):
            value = relax(own[x + 3], rhs14(x, main), inv[bx], wgt[bx], before, here, after)
            if last:
                out[x] = value
            else:
                out[x + 3] = value

        before, here = plane(low - 1), plane(low)
        for x in range(low, 0):
            after = plane(x + 1)
            write(x, 0, before, here, after)
            before, here = here, after

        def body(step, carry):
            before, here = carry
            for j in range(UNROLL):
                x = step * UNROLL + j
                after = plane(x + 1)
                write(x, (x // 8) + 1 if UNROLL > 8 else step * UNROLL // 8 + 1, before, here, after)
                before, here = here, after
            return before, here

        before, here = lax.fori_loop(0, CX // UNROLL, body, (before, here))
        for x in range(32, high + 1):
            after = plane(x + 1)
            write(x, 5, before, here, after)
            before, here = here, after

    sweep14(0, False, m0, g0, g1, False)
    sweep14(0, True, m0, g0, m1, False)
    sweep14(1, False, m1, g1, g0, False)
    sweep14(1, True, m1, g1, m0, False)
    sweep14(2, True, m0, g0, fin_out, True)


def xr_rows(ref, row):
    return ref[row : row + 16, :]


def build(interpret=False):
    def local(source, occupancy, classes, screen_table, parents, coarse):
        def sds(*shape):
            return jax.ShapeDtypeStruct(shape, F32)

        vm = pl.BlockSpec(memory_space=VMEM)
        sm = pl.BlockSpec(memory_space=SMEM)

        def send(block, axis, step):
            count = lax.axis_size(axis)
            if step > 0:
                pairs = [(i, i + step) for i in range(count - step)]
            else:
                pairs = [(i, i + step) for i in range(-step, count)]
            return lax.ppermute(block, axis, pairs)

        fl = send(coarse, "slab", 2)
        fr = send(coarse, "slab", -2)
        zl, zr, pown = pl.pallas_call(
            pack_z,
            out_shape=(sds(Z_ROWS, LANES), sds(Z_ROWS, LANES), sds(32, LANES)),
            in_specs=[vm, vm, vm, sm, sm, vm],
            out_specs=(vm, vm, vm),
            interpret=interpret,
            compiler_params=pltpu.CompilerParams(vmem_limit_bytes=4 << 20),
            name="pack_z",
        )(source, occupancy, classes, screen_table, parents, coarse)
        hl = send(zr, "slab", 1)
        hr = send(zl, "slab", -1)
        xl, xr, start, mid, ghost, bricks = pl.pallas_call(
            extend_z,
            out_shape=(
                sds(X_ROWS, LANES), sds(X_ROWS, LANES), sds(LANES, LANES), sds(16, 16, LANES),
                sds(CX, NY, LANES), sds(32, LANES),
            ),
            in_specs=[vm, sm] + [vm] * 6,
            out_specs=(vm,) * 6,
            scratch_shapes=[VMEM((24, 512), F32), VMEM((256, 2 * LANES), F32)],
            interpret=interpret,
            compiler_params=pltpu.CompilerParams(vmem_limit_bytes=8 << 20),
            name="extend_z",
        )(source, parents, coarse, pown, hl, hr, fl, fr)
        gl = send(xr, "grp", 1)
        gr = send(xl, "grp", -1)
        return pl.pallas_call(
            sweep_all,
            out_shape=(sds(16, 16, 64), sds(CX, NY, CZ)),
            in_specs=[vm] * 7,
            out_specs=(vm, vm),
            scratch_shapes=[
                VMEM((26, 16, LANES), F32),
                VMEM((64, LANES), F32),
                VMEM((8, 16, LANES), F32),
                VMEM((8, 16, LANES), F32),
            ]
            + [VMEM((6, NY, LANES), F32)] * 4
            + [VMEM((38, NY, LANES), F32)] * 4
            + [VMEM((36, NY, LANES), F32)] * 2,
            interpret=interpret,
            compiler_params=pltpu.CompilerParams(vmem_limit_bytes=16 << 20),
            name="sweep_all",
        )(source, gl, gr, start, mid, ghost, bricks)

    return local


def solution(mesh, interpret=False):
    placed = (
        P("grp", None, "slab"),
        P("grp", None, "slab"),
        P("grp", None, "slab"),
        P(),
        P("grp", None, "slab"),
        P("grp", "slab", None),
    )
    return jax.shard_map(
        build(interpret),
        mesh=mesh,
        in_specs=placed,
        out_specs=(P("grp", None, "slab"), P("grp", None, "slab")),
        check_vma=False,
    )
```

time: 285 us -> 50.2 us (0.18)
  the two profiles are of different devices: /device:TPU:111 before, /device:TPU:110 now
where the time goes in v1:
time: 50.2 us; the launch traced here: 49.7 us
  starting transfers between devices  20.8 us (41%)
  waiting for transfers between devices  14 us (28%)
  Pallas kernels  9.67 us (19%)
  local copies, waits for them, and re-layouts  4.47 us (9%)
  between operations  0.75 us (1%)
    ppermute x6, starting transfers between devices, send(): return lax.ppermute(block, axis, pairs)  20.8 us
    ppermute x6, waiting for transfers between devices, send(): return lax.ppermute(block, axis, pairs)  14 us
    pallas_call x1, Pallas kernels, local(): pl.pallas_call(sweep_all, out_shape=(sds(16, 16, 64), sds(CX, NY, CZ)), i...  7.34 us
    unnamed x18, local copies, waits for them, and re-layouts  4.47 us
    pallas_call x1, Pallas kernels, local(): pl.pallas_call(extend_z, out_shape=(sds(X_ROWS, LANES), sds(X_ROWS, LANES...  1.42 us
  transfers between devices with their start and end apart: 6, of which 3 were waited for; matrix products, arithmetic and copies ran while one was open for 0% of the time, Pallas kernels for 0%

profile of v1, /device:TPU:110, one launch (start us, length us, event | category | flops | bytes accessed | tf_op | source)
XLA Modules:
  0.0 49.7 jit_solution(10741508263757723420)
XLA Ops:
  0.6 0.0 copy-start
  0.6 1.0 %copy-done = f32[32,32,128]{2,1,0:T(8,128)S(1)} copy-done((f32[32,32,128]{2,1,0:T(8,128)S(1)}, f32[32,32,128]{2,1,0:T(8,128)}, u32[]{:S(2)}) %copy-start) | copy-done | bytes 524312
  1.7 0.0 copy-start.2
  1.7 0.7 %copy-done.2 = f32[1,4,512]{2,1,0:T(4,128)S(1)} copy-done((f32[1,4,512]{2,1,0:T(4,128)S(1)}, f32[1,4,512]{2,1,0:T(4,128)}, u32[]{:S(2)}) %copy-start.2) | copy-done | bytes 8216
  2.4 0.0 copy-start.4
  2.4 0.7 %copy-done.4 = s32[4,4,16]{2,1,0:T(4,128)S(1)} copy-done((s32[4,4,16]{2,1,0:T(4,128)S(1)}, s32[4,4,16]{2,1,0:T(4,128)}, u32[]{:S(2)}) %copy-start.4) | copy-done | bytes 1048
  3.1 0.0 copy-start.5
  3.1 0.7 %copy-done.5 = s32[4,4,16]{2,1,0:T(4,128)S(1)} copy-done((s32[4,4,16]{2,1,0:T(4,128)S(1)}, s32[4,4,16]{2,1,0:T(4,128)}, u32[]{:S(2)}) %copy-start.5) | copy-done | bytes 1048
  3.8 0.0 copy-start.6
  3.8 0.7 %copy-done.6 = s32[2,2,8]{2,1,0:T(2,128)S(1)} copy-done((s32[2,2,8]{2,1,0:T(2,128)S(1)}, s32[2,2,8]{2,1,0:T(2,128)}, u32[]{:S(2)}) %copy-start.6) | copy-done | bytes 152
  4.4 0.0 copy-start.8
  4.5 0.7 %copy-done.8 = f32[16]{0:T(128)S(1)} copy-done((f32[16]{0:T(128)S(1)}, f32[16]{0:T(128)}, u32[]{:S(2)}) %copy-start.8) | copy-done | bytes 88
  5.1 0.0 copy-start.1
  5.1 0.0 copy-start.3
  5.1 0.9 %pack_z.1 = (f32[120,128]{1,0:T(8,128)S(1)}, f32[120,128]{1,0:T(8,128)S(1)}, f32[32,128]{1,0:T(8,128)S(1)}) custom-call(f32[32,32,128]{2,1,0:T(8,128)S(1)} %copy-done, s32[4,4,16]{2,1,0:T(4,128)S(1)} %copy-done.4, s32[4,4,16]{2,1,0:T(4,128)S(1)} %copy-done.5, f32[16]{0:T(128)S(1)} %copy-done.8, s32[2,2,8]{2,1,0:T(2,128)S(1)} %copy-done.6, ...), custom_call_target="tpu_custom_call" | custom-call | tf_op jit(solution)/shard_map/pack_z/pallas_call | solution.py:346
  6.0 0.0 copy-start.7
  6.0 1.9 %collective-permute-start = (f32[120,128]{1,0:T(8,128)S(1)}, f32[120,128]{1,0:T(8,128)S(1)}, u32[]{:S(2)}, u32[]{:S(2)}) collective-permute-start(f32[120,128]{1,0:T(8,128)S(1)} %get-tuple-element.12), channel_id=1, source_target_pairs={{0,1},{1,2},{2,3},{3,4},{4,5},{5,6},{6,7},{7,8},{8,9},{9,10},{10,1... | collective-permute-start | bytes 184328 | tf_op jit(solution)/shard_map/ppermute | solution.py:342
  8.0 3.6 %collective-permute-start.1 = (f32[120,128]{1,0:T(8,128)S(1)}, f32[120,128]{1,0:T(8,128)S(1)}, u32[]{:S(2)}, u32[]{:S(2)}) collective-permute-start(f32[120,128]{1,0:T(8,128)S(1)} %get-tuple-element.13), channel_id=1, source_target_pairs={{1,0},{2,1},{3,2},{4,3},{5,4},{6,5},{7,6},{8,7},{9,8},{10,9},{11,1... | collective-permute-start | bytes 184328 | tf_op jit(solution)/shard_map/ppermute | solution.py:342
  11.6 7.0 %collective-permute-start.2 = (f32[1,4,512]{2,1,0:T(4,128)S(1)}, f32[1,4,512]{2,1,0:T(4,128)S(1)}, u32[]{:S(2)}, u32[]{:S(2)}) collective-permute-start(f32[1,4,512]{2,1,0:T(4,128)S(1)} %copy-done.2), channel_id=1, source_target_pairs={{0,2},{1,3},{2,4},{3,5},{4,6},{5,7},{6,8},{7,9},{8,10},{9,11},{10,... | collective-permute-start | bytes 24584 | tf_op jit(solution)/shard_map/ppermute | solution.py:342
  18.7 1.9 %collective-permute-start.3 = (f32[1,4,512]{2,1,0:T(4,128)S(1)}, f32[1,4,512]{2,1,0:T(4,128)S(1)}, u32[]{:S(2)}, u32[]{:S(2)}) collective-permute-start(f32[1,4,512]{2,1,0:T(4,128)S(1)} %copy-done.2), channel_id=1, source_target_pairs={{2,0},{3,1},{4,2},{5,3},{6,4},{7,5},{8,6},{9,7},{10,8},{11,9},{12,... | collective-permute-start | bytes 24584 | tf_op jit(solution)/shard_map/ppermute | solution.py:342
  20.6 0.0 collective-permute-done.2.fl
  20.6 5.7 %collective-permute-done.3.fr = f32[1,4,512]{2,1,0:T(4,128)S(1)} collective-permute-done((f32[1,4,512]{2,1,0:T(4,128)S(1)}, f32[1,4,512]{2,1,0:T(4,128)S(1)}, u32[]{:S(2)}, u32[]{:S(2)}) %collective-permute-start.3) | collective-permute-done | bytes 8224 | tf_op jit(solution)/shard_map/ppermute | solution.py:342
  26.3 0.0 collective-permute-done.hl
  26.3 0.0 collective-permute-done.1.hr
  26.3 0.0 copy-done.1
  26.3 0.0 copy-done.3
  26.3 0.0 copy-done.7
  26.3 1.4 %extend_z.1 = (f32[200,128]{1,0:T(8,128)S(1)}, f32[200,128]{1,0:T(8,128)S(1)}, f32[128,128]{1,0:T(8,128)S(1)}, f32[16,16,128]{2,1,0:T(8,128)S(1)}, f32[32,32,128]{2,1,0:T(8,128)S(1)}, /*index=5*/f32[32,128]{1,0:T(8,128)S(1)}) custom-call(f32[32,32,128]{2,1,0:T(8,128)S(1)} %copy-done.1, s32[2,2,8]{2,1,0:T(2,128)S(1)} %copy-done.7, ...), custom_call_target="tpu_custom_call" | custom-call | tf_op jit(solution)/shard_map/extend_z/pallas_call | solution.py:357
  27.8 4.4 %collective-permute-start.4 = (f32[200,128]{1,0:T(8,128)S(1)}, f32[200,128]{1,0:T(8,128)S(1)}, u32[]{:S(2)}, u32[]{:S(2)}) collective-permute-start(f32[200,128]{1,0:T(8,128)S(1)} %get-tuple-element.14), channel_id=1, source_target_pairs={{0,32},{32,64},{64,96},{96,128},{128,160},{160,192},{192,224},{1,3... | collective-permute-start | bytes 307208 | tf_op jit(solution)/shard_map/ppermute | solution.py:342
  32.2 1.9 %collective-permute-start.5 = (f32[200,128]{1,0:T(8,128)S(1)}, f32[200,128]{1,0:T(8,128)S(1)}, u32[]{:S(2)}, u32[]{:S(2)}) collective-permute-start(f32[200,128]{1,0:T(8,128)S(1)} %get-tuple-element.15), channel_id=1, source_target_pairs={{32,0},{64,32},{96,64},{128,96},{160,128},{192,160},{224,192},{33,... | collective-permute-start | bytes 307208 | tf_op jit(solution)/shard_map/ppermute | solution.py:342
  34.1 0.3 collective-permute-done.4.xl
  34.4 7.9 %collective-permute-done.5.xr = f32[200,128]{1,0:T(8,128)S(1)} collective-permute-done((f32[200,128]{1,0:T(8,128)S(1)}, f32[200,128]{1,0:T(8,128)S(1)}, u32[]{:S(2)}, u32[]{:S(2)}) %collective-permute-start.5) | collective-permute-done | bytes 102432 | tf_op jit(solution)/shard_map/ppermute | solution.py:342
  42.4 7.3 %sweep_all.1 = (f32[16,16,64]{2,1,0:T(8,128)}, f32[32,32,128]{2,1,0:T(8,128)}) custom-call(f32[32,32,128]{2,1,0:T(8,128)S(1)} %copy-done.1, f32[200,128]{1,0:T(8,128)S(1)} %collective-permute-done.4.xl, f32[200,128]{1,0:T(8,128)S(1)} %collective-permute-done.5.xr, f32[128,128]{1,0:T(8,128)S(1)} %get-tuple-element.16.start, ...), custom_call_target="tpu_custom_call" | custom-call | tf_op jit(solution)/shard_map/sweep_all/pallas_call | solution.py:372
Async XLA Ops:
  0.6 1.0 %copy-start = (f32[32,32,128]{2,1,0:T(8,128)S(1)}, f32[32,32,128]{2,1,0:T(8,128)}, u32[]{:S(2)}) copy-start(f32[32,32,128]{2,1,0:T(8,128)} %src.5) | copy-start | bytes 1572868
  1.7 0.7 %copy-start.2 = (f32[1,4,512]{2,1,0:T(4,128)S(1)}, f32[1,4,512]{2,1,0:T(4,128)}, u32[]{:S(2)}) copy-start(f32[1,4,512]{2,1,0:T(4,128)} %co.3) | copy-start | bytes 24580
  2.4 0.7 %copy-start.4 = (s32[4,4,16]{2,1,0:T(4,128)S(1)}, s32[4,4,16]{2,1,0:T(4,128)}, u32[]{:S(2)}) copy-start(s32[4,4,16]{2,1,0:T(4,128)} %occ.1) | copy-start | bytes 3076
  3.1 0.7 %copy-start.5 = (s32[4,4,16]{2,1,0:T(4,128)S(1)}, s32[4,4,16]{2,1,0:T(4,128)}, u32[]{:S(2)}) copy-start(s32[4,4,16]{2,1,0:T(4,128)} %cls.1) | copy-start | bytes 3076
  3.8 0.7 %copy-start.6 = (s32[2,2,8]{2,1,0:T(2,128)S(1)}, s32[2,2,8]{2,1,0:T(2,128)}, u32[]{:S(2)}) copy-start(s32[2,2,8]{2,1,0:T(2,128)} %par.3) | copy-start | bytes 388
  4.4 0.7 %copy-start.8 = (f32[16]{0:T(128)S(1)}, f32[16]{0:T(128)}, u32[]{:S(2)}) copy-start(f32[16]{0:T(128)} %tab.1) | copy-start | bytes 196
  5.1 21.2 %copy-start.1 = (f32[32,32,128]{2,1,0:T(8,128)S(1)}, f32[32,32,128]{2,1,0:T(8,128)}, u32[]{:S(2)}) copy-start(f32[32,32,128]{2,1,0:T(8,128)} %src.5) | copy-start | bytes 1572868
  5.1 21.2 %copy-start.3 = (f32[1,4,512]{2,1,0:T(4,128)S(1)}, f32[1,4,512]{2,1,0:T(4,128)}, u32[]{:S(2)}) copy-start(f32[1,4,512]{2,1,0:T(4,128)} %co.3) | copy-start | bytes 24580
  6.0 20.3 %copy-start.7 = (s32[2,2,8]{2,1,0:T(2,128)S(1)}, s32[2,2,8]{2,1,0:T(2,128)}, u32[]{:S(2)}) copy-start(s32[2,2,8]{2,1,0:T(2,128)} %par.3) | copy-start | bytes 388
  6.0 20.3 %collective-permute-start = (f32[120,128]{1,0:T(8,128)S(1)}, f32[120,128]{1,0:T(8,128)S(1)}, u32[]{:S(2)}, u32[]{:S(2)}) collective-permute-start(f32[120,128]{1,0:T(8,128)S(1)} %get-tuple-element.12), channel_id=1, source_target_pairs={{0,1},{1,2},{2,3},{3,4},{4,5},{5,6},{6,7},{7,8},{8,9},{9,10},{10,1... | collective-permute-start | bytes 184328 | tf_op jit(solution)/shard_map/ppermute | solution.py:342
  8.0 18.4 %collective-permute-start.1 = (f32[120,128]{1,0:T(8,128)S(1)}, f32[120,128]{1,0:T(8,128)S(1)}, u32[]{:S(2)}, u32[]{:S(2)}) collective-permute-start(f32[120,128]{1,0:T(8,128)S(1)} %get-tuple-element.13), channel_id=1, source_target_pairs={{1,0},{2,1},{3,2},{4,3},{5,4},{6,5},{7,6},{8,7},{9,8},{10,9},{11,1... | collective-permute-start | bytes 184328 | tf_op jit(solution)/shard_map/ppermute | solution.py:342
  11.6 9.0 %collective-permute-start.2 = (f32[1,4,512]{2,1,0:T(4,128)S(1)}, f32[1,4,512]{2,1,0:T(4,128)S(1)}, u32[]{:S(2)}, u32[]{:S(2)}) collective-permute-start(f32[1,4,512]{2,1,0:T(4,128)S(1)} %copy-done.2), channel_id=1, source_target_pairs={{0,2},{1,3},{2,4},{3,5},{4,6},{5,7},{6,8},{7,9},{8,10},{9,11},{10,... | collective-permute-start | bytes 24584 | tf_op jit(solution)/shard_map/ppermute | solution.py:342
  18.7 7.7 %collective-permute-start.3 = (f32[1,4,512]{2,1,0:T(4,128)S(1)}, f32[1,4,512]{2,1,0:T(4,128)S(1)}, u32[]{:S(2)}, u32[]{:S(2)}) collective-permute-start(f32[1,4,512]{2,1,0:T(4,128)S(1)} %copy-done.2), channel_id=1, source_target_pairs={{2,0},{3,1},{4,2},{5,3},{6,4},{7,5},{8,6},{9,7},{10,8},{11,9},{12,... | collective-permute-start | bytes 24584 | tf_op jit(solution)/shard_map/ppermute | solution.py:342
  27.8 6.7 %collective-permute-start.4 = (f32[200,128]{1,0:T(8,128)S(1)}, f32[200,128]{1,0:T(8,128)S(1)}, u32[]{:S(2)}, u32[]{:S(2)}) collective-permute-start(f32[200,128]{1,0:T(8,128)S(1)} %get-tuple-element.14), channel_id=1, source_target_pairs={{0,32},{32,64},{64,96},{96,128},{128,160},{160,192},{192,224},{1,3... | collective-permute-start | bytes 307208 | tf_op jit(solution)/shard_map/ppermute | solution.py:342
  32.2 10.2 %collective-permute-start.5 = (f32[200,128]{1,0:T(8,128)S(1)}, f32[200,128]{1,0:T(8,128)S(1)}, u32[]{:S(2)}, u32[]{:S(2)}) collective-permute-start(f32[200,128]{1,0:T(8,128)S(1)} %get-tuple-element.15), channel_id=1, source_target_pairs={{32,0},{64,32},{96,64},{128,96},{160,128},{192,160},{224,192},{33,... | collective-permute-start | bytes 307208 | tf_op jit(solution)/shard_map/ppermute | solution.py:342

commit v2 on v1

--- a/solution.py
+++ b/solution.py
@@ -44,12 +44,27 @@
     return v if shift == 0 else pltpu.roll(v, shift, v.ndim - 1)
 
 
-def pack_z(src, occ, cls, tab, par, co, zl, zr, pown):
-    first = (lax.axis_index("slab") - 1) * COARSE
+def pack_z(
+    src_hbm, occ_hbm, cls_hbm, tab_hbm, par_hbm, co_hbm, za, zb, co_out, pown,
+    src, occ, cls, tab, par, co, zl, zr, sems,
+):
+    copies = [
+        pltpu.make_async_copy(a, b, sems.at[i])
+        for i, (a, b) in enumerate(
+            ((occ_hbm, occ), (cls_hbm, cls), (tab_hbm, tab), (par_hbm, par), (co_hbm, co), (src_hbm, src))
+        )
+    ]
+    for copy in copies:
+        copy.start()
+    slab = lax.axis_index("slab")
+    first = (slab - 1) * COARSE
+    for copy in copies[:-1]:
+        copy.wait()
     for t in range(4):
         part = co[0, :, LANES * t : LANES * (t + 1)]
         zl[Z_COARSE + 4 * t : Z_COARSE + 4 * t + 4, :] = part
         zr[Z_COARSE + 4 * t : Z_COARSE + 4 * t + 4, :] = part
+        co_out[4 * t : 4 * t + 4, :] = part
     zl[Z_POS : Z_POS + 8, :] = jnp.full((8, LANES), par[0, 0, 0] - first, jnp.int32).astype(F32)
     zr[Z_POS : Z_POS + 8, :] = jnp.full((8, LANES), par[0, 0, 7] - first, jnp.int32).astype(F32)
     pown[...] = jnp.zeros((32, LANES), F32)
@@ -66,6 +81,7 @@
     lane = iota((32, LANES), 1)
     zl[Z_BRICK : Z_BRICK + 32, :] = jnp.where((lane == 16) | (lane == 17), turn(bricks, 16), 0.0)
     zr[Z_BRICK : Z_BRICK + 32, :] = jnp.where(lane >= 126, turn(bricks, 112), 0.0)
+    copies[-1].wait()
     slot = iota((NY, LANES), 1) // 8
     for g in range(2):
         left = jnp.zeros((NY, LANES), F32)
@@ -76,15 +92,35 @@
             right = jnp.where(slot == i, turn(v, 8 * i + 8), right)
         zl[Z_SRC + NY * g : Z_SRC + NY * (g + 1), :] = left
         zr[Z_SRC + NY * g : Z_SRC + NY * (g + 1), :] = right
-
-
-def extend_z(src, par, co, pown, hl, hr, fl, fr, xl, xr, start, mid, ghost, bricks, cand, pairs):
-    first = (lax.axis_index("slab") - 2) * COARSE
+    even = slab % 2 == 0
+    za[...] = jnp.where(even, zr[...], zl[...])
+    zb[...] = jnp.where(even, zl[...], zr[...])
+
+
+def extend_z(
+    src, par, co, pown, ha, hb, fc, fd, xa, xb, start, mid, ghost, bricks, cand, pairs, hl, hr, xl, xr
+):
+    slab = lax.axis_index("slab")
+    first = (slab - 2) * COARSE
+    even = slab % 2 == 0
+    hl[...] = jnp.where(even, hb[...], ha[...])
+    hr[...] = jnp.where(even, ha[...], hb[...])
+
+    @pl.when(slab == 0)
+    def _():
+        hl[Z_BRICK : Z_BRICK + 32, :] = jnp.zeros((32, LANES), F32)
+
+    @pl.when(slab == lax.axis_size("slab") - 1)
+    def _():
+        hr[Z_BRICK : Z_BRICK + 32, :] = jnp.zeros((32, LANES), F32)
+
+    near = slab % 4 < 2
     cand[20:24, :] = jnp.zeros((4, 512), F32)
-    cand[0:4, :] = fl[0]
     cand[8:12, :] = co[0]
-    cand[16:20, :] = fr[0]
     for t in range(4):
+        c, d = fc[4 * t : 4 * t + 4, :], fd[4 * t : 4 * t + 4, :]
+        cand[0:4, LANES * t : LANES * (t + 1)] = jnp.where(near, d, c)
+        cand[16:20, LANES * t : LANES * (t + 1)] = jnp.where(near, c, d)
         cand[4:8, LANES * t : LANES * (t + 1)] = hl[Z_COARSE + 4 * t : Z_COARSE + 4 * t + 4, :]
         cand[12:16, LANES * t : LANES * (t + 1)] = hr[Z_COARSE + 4 * t : Z_COARSE + 4 * t + 4, :]
     sub, lane = iota((8, LANES), 0), iota((8, LANES), 1)
@@ -151,6 +187,9 @@
         out[X_GHOST : X_GHOST + 8, :] = packed
         out[X_BRICK : X_BRICK + 8, :] = bricks[4 * b0 : 4 * b0 + 8, :]
         out[X_BRICK + 8 : X_BRICK + 16, :] = bricks[16 + 4 * b0 : 24 + 4 * b0, :]
+    grp_even = lax.axis_index("grp") % 2 == 0
+    xa[...] = jnp.where(grp_even, xr[...], xl[...])
+    xb[...] = jnp.where(grp_even, xl[...], xr[...])
 
 
 def up_down(v):
@@ -175,9 +214,22 @@
 
 
 def sweep_all(
-    src, xl, xr, start, smid, sghost, bricks, mid_out, fin_out,
-    v13, pext, i13, w13, i14, w14, i14g, w14g, m0, g0, m1, g1, fine, fghost,
+    src, xa, xb, start, smid, sghost, bricks, mid_out, fin_out,
+    v13, pext, i13, w13, i14, w14, i14g, w14g, m0, g0, m1, g1, fine, fghost, xl, xr,
 ):
+    grp = lax.axis_index("grp")
+    even = grp % 2 == 0
+    xl[...] = jnp.where(even, xb[...], xa[...])
+    xr[...] = jnp.where(even, xa[...], xb[...])
+
+    @pl.when(grp == 0)
+    def _():
+        xl[X_BRICK : X_BRICK + 16, :] = jnp.zeros((16, LANES), F32)
+
+    @pl.when(grp == lax.axis_size("grp") - 1)
+    def _():
+        xr[X_BRICK : X_BRICK + 16, :] = jnp.zeros((16, LANES), F32)
+
     pext[0:8, :] = xl[X_BRICK : X_BRICK + 8, :]
     pext[8:24, :] = bricks[0:16, :]
     pext[24:32, :] = xr[X_BRICK : X_BRICK + 8, :]
@@ -325,36 +377,69 @@
     return ref[row : row + 16, :]
 
 
-def build(interpret=False):
+def pairing(couples):
+    partner = {}
+    for a, b in couples:
+        partner[a], partner[b] = b, a
+    return sorted(partner.items())
+
+
+def pairings(groups, slabs):
+    def at(g, s):
+        return g * slabs + s
+
+    every = range(groups)
+    one = [(at(g, s), at(g, s + 1)) for g in every for s in range(0, slabs, 2)]
+    two = [(at(g, s), at(g, s + 1)) for g in every for s in range(1, slabs - 1, 2)]
+    two += [(at(g, s), at(g + 1, s)) for g in range(0, groups, 2) for s in (0, slabs - 1)]
+    three = [(at(g, s), at(g, s + 2)) for g in every for s in range(slabs) if s % 4 < 2]
+    four = [(at(g, s), at(g, s + 2)) for g in every for s in range(slabs - 2) if s % 4 >= 2]
+    four += [(at(g, s), at(g, s + 1)) for g in every for s in (0, slabs - 2)]
+    five = [(at(g, s), at(g + 1, s)) for g in range(0, groups, 2) for s in range(slabs)]
+    six = [(at(g, s), at(g + 1, s)) for g in range(1, groups - 1, 2) for s in range(slabs)]
+    six += [(at(g, s), at(g, s + 1)) for g in (0, groups - 1) for s in range(0, slabs, 2)]
+    return [pairing(couples) for couples in (one, two, three, four, five, six)]
+
+
+def build(mesh, interpret=False):
+    one, two, three, four, five, six = pairings(mesh.shape["grp"], mesh.shape["slab"])
+
     def local(source, occupancy, classes, screen_table, parents, coarse):
         def sds(*shape):
             return jax.ShapeDtypeStruct(shape, F32)
 
         vm = pl.BlockSpec(memory_space=VMEM)
         sm = pl.BlockSpec(memory_space=SMEM)
-
-        def send(block, axis, step):
-            count = lax.axis_size(axis)
-            if step > 0:
-                pairs = [(i, i + step) for i in range(count - step)]
-            else:
-                pairs = [(i, i + step) for i in range(-step, count)]
-            return lax.ppermute(block, axis, pairs)
-
-        fl = send(coarse, "slab", 2)
-        fr = send(coarse, "slab", -2)
-        zl, zr, pown = pl.pallas_call(
+        hbm = pl.BlockSpec(memory_space=pltpu.HBM)
+
+        def swap(block, pairs):
+            return lax.ppermute(block, ("grp", "slab"), pairs)
+
+        za, zb, rows, pown = pl.pallas_call(
             pack_z,
-            out_shape=(sds(Z_ROWS, LANES), sds(Z_ROWS, LANES), sds(32, LANES)),
-            in_specs=[vm, vm, vm, sm, sm, vm],
-            out_specs=(vm, vm, vm),
+            out_shape=(sds(Z_ROWS, LANES), sds(Z_ROWS, LANES), sds(16, LANES), sds(32, LANES)),
+            in_specs=[hbm] * 6,
+            out_specs=(vm,) * 4,
+            scratch_shapes=[
+                VMEM((CX, NY, LANES), F32),
+                VMEM((4, 4, 16), jnp.int32),
+                VMEM((4, 4, 16), jnp.int32),
+                SMEM((16,), F32),
+                SMEM((2, 2, 8), jnp.int32),
+                VMEM((1, 4, 512), F32),
+                VMEM((Z_ROWS, LANES), F32),
+                VMEM((Z_ROWS, LANES), F32),
+                pltpu.SemaphoreType.DMA((6,)),
+            ],
             interpret=interpret,
             compiler_params=pltpu.CompilerParams(vmem_limit_bytes=4 << 20),
             name="pack_z",
-        )(source, occupancy, classes, screen_table, parents, coarse)
-        hl = send(zr, "slab", 1)
-        hr = send(zl, "slab", -1)
-        xl, xr, start, mid, ghost, bricks = pl.pallas_call(
+        )(*(pltpu.with_memory_space_constraint(x, pltpu.HBM) for x in (source, occupancy, classes, screen_table, parents, coarse)))
+        ha = swap(za, one)
+        hb = swap(zb, two)
+        fc = swap(rows, three)
+        fd = swap(rows, four)
+        xa, xb, start, mid, ghost, bricks = pl.pallas_call(
             extend_z,
             out_shape=(
                 sds(X_ROWS, LANES), sds(X_ROWS, LANES), sds(LANES, LANES), sds(16, 16, LANES),
@@ -362,13 +447,20 @@
             ),
             in_specs=[vm, sm] + [vm] * 6,
             out_specs=(vm,) * 6,
-            scratch_shapes=[VMEM((24, 512), F32), VMEM((256, 2 * LANES), F32)],
+            scratch_shapes=[
+                VMEM((24, 512), F32),
+                VMEM((256, 2 * LANES), F32),
+                VMEM((Z_ROWS, LANES), F32),
+                VMEM((Z_ROWS, LANES), F32),
+                VMEM((X_ROWS, LANES), F32),
+                VMEM((X_ROWS, LANES), F32),
+            ],
             interpret=interpret,
             compiler_params=pltpu.CompilerParams(vmem_limit_bytes=8 << 20),
             name="extend_z",
-        )(source, parents, coarse, pown, hl, hr, fl, fr)
-        gl = send(xr, "grp", 1)
-        gr = send(xl, "grp", -1)
+        )(source, parents, coarse, pown, ha, hb, fc, fd)
+        ga = swap(xa, five)
+        gb = swap(xb, six)
         return pl.pallas_call(
             sweep_all,
             out_shape=(sds(16, 16, 64), sds(CX, NY, CZ)),
@@ -382,11 +474,12 @@
             ]
             + [VMEM((6, NY, LANES), F32)] * 4
             + [VMEM((38, NY, LANES), F32)] * 4
-            + [VMEM((36, NY, LANES), F32)] * 2,
+            + [VMEM((36, NY, LANES), F32)] * 2
+            + [VMEM((X_ROWS, LANES), F32)] * 2,
             interpret=interpret,
             compiler_params=pltpu.CompilerParams(vmem_limit_bytes=16 << 20),
             name="sweep_all",
-        )(source, gl, gr, start, mid, ghost, bricks)
+        )(source, ga, gb, start, mid, ghost, bricks)
 
     return local
 
@@ -401,7 +494,7 @@
         P("grp", "slab", None),
     )
     return jax.shard_map(
-        build(interpret),
+        build(mesh, interpret),
         mesh=mesh,
         in_specs=placed,
         out_specs=(P("grp", None, "slab"), P("grp", None, "slab")),

time: 50.2 us -> 29.1 us (0.58)
  the two profiles are of different devices: /device:TPU:110 before, /device:TPU:120 now
where the time goes in v2:
time: 29.1 us; the launch traced here: 29 us
  Pallas kernels  10.3 us (35%)
  waiting for transfers between devices  9.26 us (32%)
  starting transfers between devices  8.67 us (30%)
  between operations  0.7 us (2%)
    ppermute x6, waiting for transfers between devices, swap(): return lax.ppermute(block, ('grp', 'slab'), pairs)  9.26 us
    ppermute x6, starting transfers between devices, swap(): return lax.ppermute(block, ('grp', 'slab'), pairs)  8.67 us
    pallas_call x1, Pallas kernels, local(): pl.pallas_call(sweep_all, out_shape=(sds(16, 16, 64), sds(CX, NY, CZ)), i...  7.38 us
    pallas_call x1, Pallas kernels, local(): pl.pallas_call(pack_z, out_shape=(sds(Z_ROWS, LANES), sds(Z_ROWS, LANES),...  1.52 us
    pallas_call x1, Pallas kernels, local(): pl.pallas_call(extend_z, out_shape=(sds(X_ROWS, LANES), sds(X_ROWS, LANES...  1.44 us
  transfers between devices with their start and end apart: 6, of which 4 were waited for; matrix products, arithmetic and copies ran while one was open for 0% of the time, Pallas kernels for 0%

profile of v2, /device:TPU:120, one launch (start us, length us, event | category | flops | bytes accessed | tf_op | source)
XLA Modules:
  0.0 29.0 jit_solution(12064457343865233294)
XLA Ops:
  0.6 0.0 copy-start
  0.6 0.0 copy-start.1
  0.7 1.5 %pack_z.1 = (f32[120,128]{1,0:T(8,128)S(1)}, f32[120,128]{1,0:T(8,128)S(1)}, f32[16,128]{1,0:T(8,128)S(1)}, f32[32,128]{1,0:T(8,128)S(1)}) custom-call(f32[32,32,128]{2,1,0:T(8,128)} %src.3, s32[4,4,16]{2,1,0:T(4,128)} %occ_hbm.1, s32[4,4,16]{2,1,0:T(4,128)} %cls_hbm.1, f32[16]{0:T(128)} %tab_hbm.1, s32[2,2,8]{2,1,0:T(2,128)} %par.1, f32[1,4,512]{2,1,0:T(4,128)} %co.1), custom_call_target="tpu_custom_call" | custom-call | tf_op jit(solution)/shard_map/pack_z/pallas_call | solution.py:418
  2.2 0.1 collective-permute-start
  2.3 0.0 copy-start.2
  2.3 0.8 %collective-permute-start.1 = (f32[120,128]{1,0:T(8,128)S(1)}, f32[120,128]{1,0:T(8,128)S(1)}, u32[]{:S(2)}, u32[]{:S(2)}) collective-permute-start(f32[120,128]{1,0:T(8,128)S(1)} %get-tuple-element.14), channel_id=1, source_target_pairs={{0,32},{1,2},{2,1},{3,4},{4,3},{5,6},{6,5},{7,8},{8,7},{9,10},{10,... | collective-permute-start | bytes 184328 | tf_op jit(solution)/shard_map/ppermute | solution.py:416
  3.1 3.4 %collective-permute-start.3 = (f32[16,128]{1,0:T(8,128)S(1)}, f32[16,128]{1,0:T(8,128)S(1)}, u32[]{:S(2)}, u32[]{:S(2)}) collective-permute-start(f32[16,128]{1,0:T(8,128)S(1)} %get-tuple-element.15), channel_id=1, source_target_pairs={{0,1},{1,0},{2,4},{3,5},{4,2},{5,3},{6,8},{7,9},{8,6},{9,7},{10,12... | collective-permute-start | bytes 24584 | tf_op jit(solution)/shard_map/ppermute | solution.py:416
  6.5 0.0 collective-permute-start.2
  6.5 2.4 %collective-permute-done.3.fd = f32[16,128]{1,0:T(8,128)S(1)} collective-permute-done((f32[16,128]{1,0:T(8,128)S(1)}, f32[16,128]{1,0:T(8,128)S(1)}, u32[]{:S(2)}, u32[]{:S(2)}) %collective-permute-start.3) | collective-permute-done | bytes 8224 | tf_op jit(solution)/shard_map/ppermute | solution.py:416
  8.9 1.3 %collective-permute-done.2.fc = f32[16,128]{1,0:T(8,128)S(1)} collective-permute-done((f32[16,128]{1,0:T(8,128)S(1)}, f32[16,128]{1,0:T(8,128)S(1)}, u32[]{:S(2)}, u32[]{:S(2)}) %collective-permute-start.2) | collective-permute-done | bytes 8224 | tf_op jit(solution)/shard_map/ppermute | solution.py:416
  10.2 0.0 collective-permute-done.ha
  10.2 0.0 collective-permute-done.1.hb
  10.2 0.0 copy-done
  10.2 0.0 copy-done.1
  10.2 0.0 copy-done.2
  10.2 1.4 %extend_z.1 = (f32[200,128]{1,0:T(8,128)S(1)}, f32[200,128]{1,0:T(8,128)S(1)}, f32[128,128]{1,0:T(8,128)S(1)}, f32[16,16,128]{2,1,0:T(8,128)S(1)}, f32[32,32,128]{2,1,0:T(8,128)S(1)}, /*index=5*/f32[32,128]{1,0:T(8,128)S(1)}) custom-call(f32[32,32,128]{2,1,0:T(8,128)S(1)} %copy-done, s32[2,2,8]{2,1,0:T(2,128)S(1)} %copy-done.2, f32[1,4,512]{2,1,0:T(4,128)S(1)} %copy-done.1, ...), custom_call_target="tpu_custom_call" | custom-call | tf_op jit(solution)/shard_map/extend_z/pallas_call | solution.py:442
  11.7 1.6 %collective-permute-start.4 = (f32[200,128]{1,0:T(8,128)S(1)}, f32[200,128]{1,0:T(8,128)S(1)}, u32[]{:S(2)}, u32[]{:S(2)}) collective-permute-start(f32[200,128]{1,0:T(8,128)S(1)} %get-tuple-element.16), channel_id=1, source_target_pairs={{0,32},{1,33},{2,34},{3,35},{4,36},{5,37},{6,38},{7,39},{8,40},{9,... | collective-permute-start | bytes 307208 | tf_op jit(solution)/shard_map/ppermute | solution.py:416
  13.2 2.8 %collective-permute-start.5 = (f32[200,128]{1,0:T(8,128)S(1)}, f32[200,128]{1,0:T(8,128)S(1)}, u32[]{:S(2)}, u32[]{:S(2)}) collective-permute-start(f32[200,128]{1,0:T(8,128)S(1)} %get-tuple-element.17), channel_id=1, source_target_pairs={{0,1},{1,0},{2,3},{3,2},{4,5},{5,4},{6,7},{7,6},{8,9},{9,8},{10,11... | collective-permute-start | bytes 307208 | tf_op jit(solution)/shard_map/ppermute | solution.py:416
  16.0 0.8 %collective-permute-done.4.xa = f32[200,128]{1,0:T(8,128)S(1)} collective-permute-done((f32[200,128]{1,0:T(8,128)S(1)}, f32[200,128]{1,0:T(8,128)S(1)}, u32[]{:S(2)}, u32[]{:S(2)}) %collective-permute-start.4) | collective-permute-done | bytes 102432 | tf_op jit(solution)/shard_map/ppermute | solution.py:416
  16.8 4.8 %collective-permute-done.5.xb = f32[200,128]{1,0:T(8,128)S(1)} collective-permute-done((f32[200,128]{1,0:T(8,128)S(1)}, f32[200,128]{1,0:T(8,128)S(1)}, u32[]{:S(2)}, u32[]{:S(2)}) %collective-permute-start.5) | collective-permute-done | bytes 102432 | tf_op jit(solution)/shard_map/ppermute | solution.py:416
  21.6 7.4 %sweep_all.1 = (f32[16,16,64]{2,1,0:T(8,128)}, f32[32,32,128]{2,1,0:T(8,128)}) custom-call(f32[32,32,128]{2,1,0:T(8,128)S(1)} %copy-done, f32[200,128]{1,0:T(8,128)S(1)} %collective-permute-done.4.xa, f32[200,128]{1,0:T(8,128)S(1)} %collective-permute-done.5.xb, f32[128,128]{1,0:T(8,128)S(1)} %get-tuple-element.18.start, ...), custom_call_target="tpu_custom_call" | custom-call | tf_op jit(solution)/shard_map/sweep_all/pallas_call | solution.py:464
Async XLA Ops:
  0.6 9.5 %copy-start = (f32[32,32,128]{2,1,0:T(8,128)S(1)}, f32[32,32,128]{2,1,0:T(8,128)}, u32[]{:S(2)}) copy-start(f32[32,32,128]{2,1,0:T(8,128)} %src.3) | copy-start | bytes 1572868
  0.6 9.5 %copy-start.1 = (f32[1,4,512]{2,1,0:T(4,128)S(1)}, f32[1,4,512]{2,1,0:T(4,128)}, u32[]{:S(2)}) copy-start(f32[1,4,512]{2,1,0:T(4,128)} %co.1) | copy-start | bytes 24580
  2.2 8.0 %collective-permute-start = (f32[120,128]{1,0:T(8,128)S(1)}, f32[120,128]{1,0:T(8,128)S(1)}, u32[]{:S(2)}, u32[]{:S(2)}) collective-permute-start(f32[120,128]{1,0:T(8,128)S(1)} %get-tuple-element.13), channel_id=1, source_target_pairs={{0,1},{1,0},{2,3},{3,2},{4,5},{5,4},{6,7},{7,6},{8,9},{9,8},{10,11... | collective-permute-start | bytes 184328 | tf_op jit(solution)/shard_map/ppermute | solution.py:416
  2.3 7.9 %copy-start.2 = (s32[2,2,8]{2,1,0:T(2,128)S(1)}, s32[2,2,8]{2,1,0:T(2,128)}, u32[]{:S(2)}) copy-start(s32[2,2,8]{2,1,0:T(2,128)} %par.1) | copy-start | bytes 388
  2.3 7.9 %collective-permute-start.1 = (f32[120,128]{1,0:T(8,128)S(1)}, f32[120,128]{1,0:T(8,128)S(1)}, u32[]{:S(2)}, u32[]{:S(2)}) collective-permute-start(f32[120,128]{1,0:T(8,128)S(1)} %get-tuple-element.14), channel_id=1, source_target_pairs={{0,32},{1,2},{2,1},{3,4},{4,3},{5,6},{6,5},{7,8},{8,7},{9,10},{10,... | collective-permute-start | bytes 184328 | tf_op jit(solution)/shard_map/ppermute | solution.py:416
  3.1 5.8 %collective-permute-start.3 = (f32[16,128]{1,0:T(8,128)S(1)}, f32[16,128]{1,0:T(8,128)S(1)}, u32[]{:S(2)}, u32[]{:S(2)}) collective-permute-start(f32[16,128]{1,0:T(8,128)S(1)} %get-tuple-element.15), channel_id=1, source_target_pairs={{0,1},{1,0},{2,4},{3,5},{4,2},{5,3},{6,8},{7,9},{8,6},{9,7},{10,12... | collective-permute-start | bytes 24584 | tf_op jit(solution)/shard_map/ppermute | solution.py:416
  6.5 3.7 %collective-permute-start.2 = (f32[16,128]{1,0:T(8,128)S(1)}, f32[16,128]{1,0:T(8,128)S(1)}, u32[]{:S(2)}, u32[]{:S(2)}) collective-permute-start(f32[16,128]{1,0:T(8,128)S(1)} %get-tuple-element.15), channel_id=1, source_target_pairs={{0,2},{1,3},{2,0},{3,1},{4,6},{5,7},{6,4},{7,5},{8,10},{9,11},{10,... | collective-permute-start | bytes 24584 | tf_op jit(solution)/shard_map/ppermute | solution.py:416
  11.7 5.1 %collective-permute-start.4 = (f32[200,128]{1,0:T(8,128)S(1)}, f32[200,128]{1,0:T(8,128)S(1)}, u32[]{:S(2)}, u32[]{:S(2)}) collective-permute-start(f32[200,128]{1,0:T(8,128)S(1)} %get-tuple-element.16), channel_id=1, source_target_pairs={{0,32},{1,33},{2,34},{3,35},{4,36},{5,37},{6,38},{7,39},{8,40},{9,... | collective-permute-start | bytes 307208 | tf_op jit(solution)/shard_map/ppermute | solution.py:416
  13.2 8.4 %collective-permute-start.5 = (f32[200,128]{1,0:T(8,128)S(1)}, f32[200,128]{1,0:T(8,128)S(1)}, u32[]{:S(2)}, u32[]{:S(2)}) collective-permute-start(f32[200,128]{1,0:T(8,128)S(1)} %get-tuple-element.17), channel_id=1, source_target_pairs={{0,1},{1,0},{2,3},{3,2},{4,5},{5,4},{6,7},{7,6},{8,9},{9,8},{10,11... | collective-permute-start | bytes 307208 | tf_op jit(solution)/shard_map/ppermute | solution.py:416

commit v3 on v2

v3 whole, which is shorter than its diff:
```python
import jax
import jax.numpy as jnp
from jax import lax
from jax.experimental import pallas as pl
from jax.experimental.pallas import tpu as pltpu
from jax.sharding import PartitionSpec as P

BRICK = 8
SWEEPS = 3

screen_strength = 4.0
relaxation = 2.0 / 3.0
stiff_diagonal = 8.0 / 3.0
mass_diagonal = 8.0 / 27.0

F32 = jnp.float32
HI = lax.Precision.HIGHEST
VMEM = pltpu.VMEM
SMEM = pltpu.SMEM

CX, NY, CZ = 32, 32, 128
LANES = 128
COARSE = 4

Z_COARSE, Z_POS, Z_BRICK, Z_SRC, Z_ROWS = 0, 16, 24, 32, 96
X_START, X_MID, X_FINE, X_GHOST, X_BRICK, X_ROWS = 0, 24, 88, 152, 160, 168


def iota(shape, dim):
    return lax.broadcasted_iota(jnp.int32, shape, dim)


def onehot(mask):
    return jnp.where(mask, 1.0, 0.0).astype(F32)


def dot(a, b):
    return jnp.dot(a, b, precision=HI, preferred_element_type=F32)


def turn(v, shift):
    shift = shift % LANES
    return v if shift == 0 else pltpu.roll(v, shift, v.ndim - 1)


def y_sum(tiles):
    n = len(tiles)
    sub = iota((8, LANES), 0)
    first = jnp.where(sub == 0, 0.0, pltpu.roll(tiles[n - 1], 1, 0))
    last = jnp.where(sub == 7, 0.0, pltpu.roll(tiles[0], 7, 0))
    up = [first] + tiles[:-1]
    down = tiles[1:] + [last]
    return [a + b for a, b in zip(up, down)]


def along_y(tiles, z_sums):
    four = [4.0 * v for v in tiles]
    a = [v + z for v, z in zip(four, z_sums)]
    b = [v + y for v, y in zip(four, y_sum(tiles))]
    c = [4.0 * v + y for v, y in zip(a, y_sum(a))]
    return [x + y for x, y in zip(a, b)], c


def relax(v, rhs, inverse, weight, d, e, c):
    return v + inverse * ((rhs - (c + d)) - weight * e)


def along_x(before, here, after):
    return 4.0 * here + (before + after)


def pack_z(
    src_hbm, occ_hbm, cls_hbm, tab_hbm, par_hbm, co_hbm, za, zb, co_out, pown, fine,
    src, occ, cls, tab, par, co, zl, zr, sems,
):
    copies = [
        pltpu.make_async_copy(a, b, sems.at[i])
        for i, (a, b) in enumerate(
            ((occ_hbm, occ), (cls_hbm, cls), (tab_hbm, tab), (par_hbm, par), (co_hbm, co), (src_hbm, src))
        )
    ]
    for copy in copies:
        copy.start()
    slab = lax.axis_index("slab")
    first = (slab - 1) * COARSE
    for copy in copies[:-1]:
        copy.wait()
    for t in range(4):
        part = co[0, :, LANES * t : LANES * (t + 1)]
        zl[Z_COARSE + 4 * t : Z_COARSE + 4 * t + 4, :] = part
        co_out[4 * t : 4 * t + 4, :] = part
    zr[Z_COARSE : Z_COARSE + 16, :] = zl[Z_COARSE : Z_COARSE + 16, :]
    zl[Z_POS : Z_POS + 8, :] = jnp.full((8, LANES), par[0, 0, 0] - first, jnp.int32).astype(F32)
    zr[Z_POS : Z_POS + 8, :] = jnp.full((8, LANES), par[0, 0, 7] - first, jnp.int32).astype(F32)
    pown[...] = jnp.zeros((64, LANES), F32)
    for bx in range(4):
        occupied = occ[bx].astype(F32)
        labels = cls[bx]
        weight = jnp.zeros((4, 16), F32)
        for c in range(16):
            weight = weight + jnp.where(labels == c, tab[c], 0.0)
        screen = screen_strength * weight
        inverse = occupied / (stiff_diagonal + screen * mass_diagonal)
        for parity in range(2):
            pown[pl.ds(8 * bx + parity, 4, 2), 0:16] = inverse
            pown[pl.ds(32 + 8 * bx + parity, 4, 2), 0:16] = screen
    lane = iota((8, LANES), 1)
    packed = jnp.zeros((8, LANES), F32)
    for q in range(8):
        packed = jnp.where(lane // 16 == q, turn(pown[8 * q : 8 * q + 8, :], 16 * q), packed)
    zl[Z_BRICK : Z_BRICK + 8, :] = packed
    zr[Z_BRICK : Z_BRICK + 8, :] = packed
    copies[-1].wait()
    slot = lane // 8
    for g in range(2):
        for t in range(4):
            left = jnp.zeros((8, LANES), F32)
            right = jnp.zeros((8, LANES), F32)
            for i in range(16):
                v = 6.0 * src[16 * g + i, pl.ds(t, 8, 4), :]
                fine[16 * g + i, 8 * t : 8 * t + 8, :] = v
                left = jnp.where(slot == i, turn(v, 8 * i), left)
                right = jnp.where(slot == i, turn(v, 8 * i + 8), right)
            row = Z_SRC + 32 * g + 8 * t
            zl[row : row + 8, :] = left
            zr[row : row + 8, :] = right
    even = slab % 2 == 0
    za[...] = jnp.where(even, zr[...], zl[...])
    zb[...] = jnp.where(even, zl[...], zr[...])


def extend_z(
    fine, par, co, pown, ha, hb, fc, fd, xa, xb, start, mid, ghost, bricks, cand, pairs, hl, hr, xl, xr
):
    slab = lax.axis_index("slab")
    first = (slab - 2) * COARSE
    even = slab % 2 == 0
    hl[...] = jnp.where(even, hb[...], ha[...])
    hr[...] = jnp.where(even, ha[...], hb[...])

    @pl.when(slab == 0)
    def _():
        hl[Z_BRICK : Z_BRICK + 8, :] = jnp.zeros((8, LANES), F32)

    @pl.when(slab == lax.axis_size("slab") - 1)
    def _():
        hr[Z_BRICK : Z_BRICK + 8, :] = jnp.zeros((8, LANES), F32)

    near = slab % 4 < 2
    cand[20:24, :] = jnp.zeros((4, 512), F32)
    cand[8:12, :] = co[0]
    for t in range(4):
        c, d = fc[4 * t : 4 * t + 4, :], fd[4 * t : 4 * t + 4, :]
        cand[0:4, LANES * t : LANES * (t + 1)] = jnp.where(near, d, c)
        cand[16:20, LANES * t : LANES * (t + 1)] = jnp.where(near, c, d)
        cand[4:8, LANES * t : LANES * (t + 1)] = hl[Z_COARSE + 4 * t : Z_COARSE + 4 * t + 4, :]
        cand[12:16, LANES * t : LANES * (t + 1)] = hr[Z_COARSE + 4 * t : Z_COARSE + 4 * t + 4, :]
    sub, lane = iota((8, LANES), 0), iota((8, LANES), 1)
    chosen = jnp.full((8, LANES), -1, jnp.int32)
    for k in range(4):
        chosen = jnp.where(sub == k + 1, par[0, 0, 2 * k] - first, chosen)
    chosen = chosen.astype(F32)
    chosen = jnp.where(sub == 0, hl[Z_POS : Z_POS + 8, :], chosen)
    chosen = jnp.where(sub == 5, hr[Z_POS : Z_POS + 8, :] + 2.0 * COARSE, chosen)
    pick = onehot(chosen == lane.astype(F32))
    six = dot(pick[:, 0:24], cand[...])
    row2, lane2 = iota((16, LANES), 0), iota((16, LANES), 1)
    spread = onehot(lane2 // 8 == row2)
    c, z = iota((LANES, LANES), 0), iota((LANES, LANES), 1)
    place = onehot(c % 8 == z % 16 // 2)
    zone = lane2 // 16
    rows = jnp.concatenate(
        [
            jnp.broadcast_to(six[k : k + 1, LANES * t : LANES * (t + 1)], (16, LANES)) * spread
            for t in range(4)
            for k in range(6)
        ],
        axis=0,
    )
    placed = dot(rows, place)
    for t in range(4):
        total = jnp.zeros((16, LANES), F32)
        for k in range(6):
            at = 16 * (6 * t + k)
            total = jnp.where(zone == (7 if k == 0 else k - 1), placed[at : at + 16], total)
        start[16 * t : 16 * (t + 1), :] = total
    for q in range(8):
        low = turn(hl[Z_BRICK : Z_BRICK + 8, :], 112 - 16 * q)
        high = turn(hr[Z_BRICK : Z_BRICK + 8, :], 16 - 16 * q)
        own = pown[8 * q : 8 * q + 8, :]
        bricks[8 * q : 8 * q + 8, :] = jnp.where(lane >= 126, low, jnp.where(lane // 2 == 8, high, own))
    for g in range(2):
        for t in range(4):
            row = Z_SRC + 32 * g + 8 * t
            low, high = turn(hl[row : row + 8, :], -4), turn(hr[row : row + 8, :], 4)
            ghost[32 * g + 8 * t : 32 * g + 8 * t + 8, :] = jnp.where(lane % 8 < 4, low, high)
    z2, l2 = iota((2 * LANES, LANES), 0), iota((2 * LANES, LANES), 1)
    join = (z2 < 128) & (z2 // 2 == l2)
    join = join | ((z2 >= 128) & (z2 < 136) & (l2 == 64 + (z2 - 128) // 2))
    join = join | ((z2 >= 248) & (l2 == z2 // 2))
    join = onehot(join)
    for g in range(2):
        for u in range(2):
            row = Z_SRC + 32 * g + 16 * u
            low = hl[row : row + 8, :] + hl[row + 8 : row + 16, :]
            high = hr[row : row + 8, :] + hr[row + 8 : row + 16, :]
            low, high = low + turn(low, -8), high + turn(high, -8)
            for i in range(8):
                x, at = 2 * (8 * g + i), 16 * (8 * g + i) + 8 * u
                pairs[at : at + 8, 0:LANES] = (
                    fine[x, 16 * u : 16 * u + 8, :]
                    + fine[x, 16 * u + 8 : 16 * u + 16, :]
                    + fine[x + 1, 16 * u : 16 * u + 8, :]
                    + fine[x + 1, 16 * u + 8 : 16 * u + 16, :]
                )
                pairs[at : at + 8, LANES:] = jnp.where(
                    lane < 8, turn(high, -16 * i), jnp.where(lane >= 120, turn(low, 120 - 16 * i), 0.0)
                )
    summed = 0.25 * dot(pairs[...], join)
    for i in range(16):
        mid[i] = summed[16 * i : 16 * (i + 1)]
    for out, rows, m0, f0, g0, b0, edge in ((xl, 0, 0, 0, 0, 0, 0), (xr, 40, 12, 30, 1, 2, 16)):
        out[X_START : X_START + 24, :] = start[rows : rows + 24, :]
        for i in range(4):
            out[X_MID + 16 * i : X_MID + 16 * (i + 1), :] = mid[m0 + i]
        for i in range(2):
            out[X_FINE + NY * i : X_FINE + NY * (i + 1), :] = fine[f0 + i]
        packed = jnp.zeros((8, LANES), F32)
        boxes = jnp.zeros((8, LANES), F32)
        for t in range(4):
            v = ghost[32 * g0 + 8 * t : 32 * g0 + 8 * t + 8, :]
            packed = jnp.where(lane // 16 == t, turn(v, 16 * t + edge), packed)
            at = 32 * (t // 2) + 8 * (b0 + t % 2)
            boxes = jnp.where(lane // 32 == t, turn(bricks[at : at + 8, :], 32 * t + 2), boxes)
        out[X_GHOST : X_GHOST + 8, :] = packed
        out[X_BRICK : X_BRICK + 8, :] = boxes
    grp_even = lax.axis_index("grp") % 2 == 0
    xa[...] = jnp.where(grp_even, xr[...], xl[...])
    xb[...] = jnp.where(grp_even, xl[...], xr[...])


def sweep_all(
    fine, xa, xb, start, smid, sghost, bricks, mid_hbm, fin_hbm,
    v13, pext, coef, rep, m1, m2, xl, xr, mid_out, fin_out, sems,
):
    grp = lax.axis_index("grp")
    even = grp % 2 == 0
    xl[...] = jnp.where(even, xb[...], xa[...])
    xr[...] = jnp.where(even, xa[...], xb[...])

    @pl.when(grp == 0)
    def _():
        xl[X_BRICK : X_BRICK + 8, :] = jnp.zeros((8, LANES), F32)

    @pl.when(grp == lax.axis_size("grp") - 1)
    def _():
        xr[X_BRICK : X_BRICK + 8, :] = jnp.zeros((8, LANES), F32)

    lane = iota((8, LANES), 1)
    ring = (lane < 18) | (lane >= 126)
    for field in range(2):
        pext[64 * field + 16 : 64 * field + 48, :] = bricks[32 * field : 32 * field + 32, :]
        for b in range(2):
            shift = -(32 * (2 * field + b) + 2)
            at = 64 * field + 8 * b
            pext[at : at + 8, :] = jnp.where(ring, turn(xl[X_BRICK : X_BRICK + 8, :], shift), 0.0)
            pext[at + 48 : at + 56, :] = jnp.where(ring, turn(xr[X_BRICK : X_BRICK + 8, :], shift), 0.0)
    b, l = iota((LANES, 3 * LANES), 0), iota((LANES, 3 * LANES), 1)
    z = l % LANES
    hit = (l < 128) & (b == jnp.where(z >= 96, z // 4 + 96, z // 4))
    hit = hit | ((l >= 128) & (l < 256) & (b == z // 8))
    hit = hit | ((l >= 256) & (b == jnp.where(z % 8 < 4, 127, 16)))
    spread = dot(pext[...], onehot(hit))
    coef[0:64, :] = spread[0:64] * (relaxation / 6.0)
    coef[64:128, :] = spread[64:128] * (1.0 / 36.0) - 0.5

    def inverse13(bx):
        return coef[8 * (bx + 2) : 8 * (bx + 3), 0:LANES]

    def weight13(bx):
        return coef[64 + 8 * (bx + 2) : 72 + 8 * (bx + 2), 0:LANES]

    def inverse14(bx):
        return coef[8 * (bx + 2) : 8 * (bx + 3), LANES : 2 * LANES]

    def weight14(bx):
        return coef[64 + 8 * (bx + 2) : 72 + 8 * (bx + 2), LANES : 2 * LANES]

    for x in range(-5, 21):
        q = x // 2
        if q < 0:
            v = xl[X_START + 8 * (q + 3) : X_START + 8 * (q + 4), :]
        elif q > 7:
            v = xr[X_START + 8 * (q - 8) : X_START + 8 * (q - 7), :]
        else:
            v = start[8 * q : 8 * q + 8, :]
        v = jnp.where(inverse13(x // 4) != 0.0, v, 0.0)
        v13[x + 5, 0:8, :] = v
        v13[x + 5, 8:16, :] = v

    def rhs13(x, u):
        if x < 0:
            return xl[X_MID + 16 * (x + 4) + 8 * u : X_MID + 16 * (x + 4) + 8 * u + 8, :]
        if x > 15:
            return xr[X_MID + 16 * (x - 16) + 8 * u : X_MID + 16 * (x - 16) + 8 * u + 8, :]
        return smid[x, 8 * u : 8 * u + 8, :]

    for n in range(SWEEPS):
        low, high = -4 + n, 19 - n
        planes = {}
        for x in range(low - 1, high + 2):
            tiles = [v13[x + 5, 8 * u : 8 * u + 8, :] for u in range(2)]
            planes[x] = along_y(tiles, [turn(v, 1) + turn(v, -1) for v in tiles])
            if x > low:
                o = x - 1
                for u in range(2):
                    d = along_x(planes[o - 1][0][u], planes[o][0][u], planes[x][0][u])
                    e = along_x(planes[o - 1][1][u], planes[o][1][u], planes[x][1][u])
                    v13[o + 5, 8 * u : 8 * u + 8, :] = relax(
                        v13[o + 5, 8 * u : 8 * u + 8, :],
                        rhs13(o, u), inverse13(o // 4), weight13(o // 4), d, e, planes[o][1][u],
                    )
    for x in range(16):
        for u in range(2):
            mid_out[x, pl.ds(u, 8, 2), :] = v13[x + 5, 8 * u : 8 * u + 8, 0:64]
    mid_copy = pltpu.make_async_copy(mid_out, mid_hbm, sems.at[0])
    mid_copy.start()

    b, l = iota((LANES, 2 * LANES), 0), iota((LANES, 2 * LANES), 1)
    j = l % 8
    hit = (l < 128) & (b == l // 2)
    hit = hit | ((l >= 128) & (b == jnp.where(j < 4, 126 + j // 2, 62 + j // 2)))
    parents = jnp.concatenate(
        [
            jnp.where(inverse13(x // 4) != 0.0, v13[x + 5, 8 * u : 8 * u + 8, :], 0.0)
            for x in range(-2, 18)
            for u in range(2)
        ],
        axis=0,
    )
    rep[...] = dot(parents, onehot(hit))

    def parent(q, u):
        return rep[16 * (q + 2) + 8 * u : 16 * (q + 2) + 8 * u + 8, 0:LANES]

    zero = jnp.zeros((8, LANES), F32)
    halo = [[zero, zero] for _ in range(4)]
    for q in range(-2, 18):
        g, i = q // 8 + 1, q % 8
        for u in range(2):
            v = rep[16 * (q + 2) + 8 * u : 16 * (q + 2) + 8 * u + 8, LANES:]
            halo[g][u] = jnp.where(lane // 16 == i, v, halo[g][u])
    halo = [[tiles[t // 2] for t in range(4)] for tiles in halo]
    halo_rhs, halo_inverse, halo_weight = [], [], []
    for g in range(4):
        if g == 0:
            packed = xl[X_GHOST : X_GHOST + 8, :]
            halo_rhs.append([turn(packed, 112 - 16 * t) for t in range(4)])
        elif g == 3:
            packed = xr[X_GHOST : X_GHOST + 8, :]
            halo_rhs.append([turn(packed, -16 * t) for t in range(4)])
        else:
            halo_rhs.append([sghost[32 * (g - 1) + 8 * t : 32 * (g - 1) + 8 * t + 8, :] for t in range(4)])
        for field, out in ((0, halo_inverse), (64, halo_weight)):
            one, two = (coef[field + 8 * (2 * g + k) : field + 8 * (2 * g + k) + 8, 2 * LANES :] for k in range(2))
            out.append(jnp.where(lane < 64, one, two))

    def z_main(v, halo_tile, i):
        edge = turn(halo_tile, -(8 * i + 4))
        return turn(jnp.where(lane == 127, edge, v), 1) + turn(jnp.where(lane == 0, edge, v), -1)

    def sweep_halo(halo, edges):
        planes = []
        for g in range(4):
            right = [jnp.where(lane % 8 == 3, e, v) for e, v in zip(edges[g], halo[g])]
            left = [jnp.where(lane % 8 == 4, e, v) for e, v in zip(edges[g], halo[g])]
            planes.append(along_y(halo[g], [turn(r, 1) + turn(v, -1) for r, v in zip(right, left)]))
        moved = [[[(turn(v, 8), turn(v, -8)) for v in part] for part in plane] for plane in planes]
        out = []
        for g in range(4):
            tiles = []
            for t in range(4):
                de = []
                for part in range(2):
                    before, after = moved[g][part][t]
                    if g > 0:
                        before = jnp.where(lane < 8, moved[g - 1][part][t][0], before)
                    if g < 3:
                        after = jnp.where(lane >= 120, moved[g + 1][part][t][1], after)
                    de.append(along_x(before, planes[g][part][t], after))
                tiles.append(
                    relax(
                        halo[g][t], halo_rhs[g][t], halo_inverse[g], halo_weight[g],
                        de[0], de[1], planes[g][1][t],
                    )
                )
            out.append(tiles)
        return out

    def rhs14(x, t):
        if x < 0:
            return xl[X_FINE + NY * (x + 2) + 8 * t : X_FINE + NY * (x + 2) + 8 * t + 8, :]
        if x > 31:
            return xr[X_FINE + NY * (x - 32) + 8 * t : X_FINE + NY * (x - 32) + 8 * t + 8, :]
        return fine[x, 8 * t : 8 * t + 8, :]

    edges = [[zero, zero] for _ in range(4)]
    for q in range(-2, 18):
        for child in range(2):
            g, i = (2 * q) // 16 + 1, (2 * q) % 16 + child
            for u in range(2):
                edges[g][u] = jnp.where(lane // 8 == i, turn(parent(q, u), 8 * i + 4), edges[g][u])
    edges = [[tiles[t // 2] for t in range(4)] for tiles in edges]
    planes = {}
    for q in range(-2, 18):
        g, i = (2 * q) // 16 + 1, (2 * q) % 16
        tiles = [parent(q, u) for u in range(2)]
        sums = [z_main(tiles[u], halo[g][2 * u], i) for u in range(2)]
        planes[q] = along_y([tiles[t // 2] for t in range(4)], [sums[t // 2] for t in range(4)])
        o = q - 1
        if o >= -1:
            for t in range(4):
                f5, c5 = 5.0 * planes[o][0][t], 5.0 * planes[o][1][t]
                for child in range(2):
                    x, near = 2 * o + child, o - 1 + 2 * child
                    d, e = f5 + planes[near][0][t], c5 + planes[near][1][t]
                    m1[x + 3, 8 * t : 8 * t + 8, :] = relax(
                        parent(o, t // 2), rhs14(x, t), inverse14(x // 8), weight14(x // 8),
                        d, e, planes[o][1][t],
                    )
    halo = sweep_halo(halo, edges)

    pieces = []
    for n, source, target in ((1, m1, m2), (2, m2, None)):
        low, high = -2 + n, 33 - n
        if n == 1:
            edges = [[zero] * 4 for _ in range(4)]
            for x in range(low - 1, high + 2):
                g, i = x // 16 + 1, x % 16
                for t in range(4):
                    v = source[x + 3, 8 * t : 8 * t + 8, :]
                    edges[g][t] = jnp.where(lane // 8 == i, turn(v, 8 * i + 4), edges[g][t])
        planes = {}
        for x in range(low - 1, high + 2):
            g, i = x // 16 + 1, x % 16
            tiles = [source[x + 3, 8 * t : 8 * t + 8, :] for t in range(4)]
            planes[x] = along_y(tiles, [z_main(tiles[t], halo[g][t], i) for t in range(4)])
            if x > low:
                o = x - 1
                for t in range(4):
                    d = along_x(planes[o - 1][0][t], planes[o][0][t], planes[x][0][t])
                    e = along_x(planes[o - 1][1][t], planes[o][1][t], planes[x][1][t])
                    value = relax(
                        source[o + 3, 8 * t : 8 * t + 8, :],
                        rhs14(o, t), inverse14(o // 8), weight14(o // 8), d, e, planes[o][1][t],
                    )
                    if target is None:
                        fin_out[o, pl.ds(t, 8, 4), :] = value
                    else:
                        target[o + 3, 8 * t : 8 * t + 8, :] = value
                if target is None and o % 8 == 7:
                    part = pl.ds(o - 7, 8)
                    pieces.append(pltpu.make_async_copy(fin_out.at[part], fin_hbm.at[part], sems.at[1 + o // 8]))
                    pieces[-1].start()
        if n == 1:
            halo = sweep_halo(halo, edges)
    mid_copy.wait()
    for piece in pieces:
        piece.wait()


def pairing(couples):
    partner = {}
    for a, b in couples:
        partner[a], partner[b] = b, a
    return sorted(partner.items())


def pairings(groups, slabs):
    def at(g, s):
        return g * slabs + s

    every = range(groups)
    one = [(at(g, s), at(g, s + 1)) for g in every for s in range(0, slabs, 2)]
    two = [(at(g, s), at(g, s + 1)) for g in every for s in range(1, slabs - 1, 2)]
    two += [(at(g, s), at(g + 1, s)) for g in range(0, groups, 2) for s in (0, slabs - 1)]
    three = [(at(g, s), at(g, s + 2)) for g in every for s in range(slabs) if s % 4 < 2]
    four = [(at(g, s), at(g, s + 2)) for g in every for s in range(slabs - 2) if s % 4 >= 2]
    four += [(at(g, s), at(g, s + 1)) for g in every for s in (0, slabs - 2)]
    five = [(at(g, s), at(g + 1, s)) for g in range(0, groups, 2) for s in range(slabs)]
    six = [(at(g, s), at(g + 1, s)) for g in range(1, groups - 1, 2) for s in range(slabs)]
    six += [(at(g, s), at(g, s + 1)) for g in (0, groups - 1) for s in range(0, slabs, 2)]
    return [pairing(couples) for couples in (one, two, three, four, five, six)]


def build(mesh, interpret=False):
    one, two, three, four, five, six = pairings(mesh.shape["grp"], mesh.shape["slab"])

    def local(source, occupancy, classes, screen_table, parents, coarse):
        def sds(*shape):
            return jax.ShapeDtypeStruct(shape, F32)

        vm = pl.BlockSpec(memory_space=VMEM)
        sm = pl.BlockSpec(memory_space=SMEM)
        hbm = pl.BlockSpec(memory_space=pltpu.HBM)

        def swap(block, pairs):
            return lax.ppermute(block, ("grp", "slab"), pairs)

        za, zb, rows, pown, fine = pl.pallas_call(
            pack_z,
            out_shape=(
                sds(Z_ROWS, LANES), sds(Z_ROWS, LANES), sds(16, LANES), sds(64, LANES), sds(CX, NY, LANES),
            ),
            in_specs=[hbm] * 6,
            out_specs=(vm,) * 5,
            scratch_shapes=[
                VMEM((CX, NY, LANES), F32),
                VMEM((4, 4, 16), jnp.int32),
                VMEM((4, 4, 16), jnp.int32),
                SMEM((16,), F32),
                SMEM((2, 2, 8), jnp.int32),
                VMEM((1, 4, 512), F32),
                VMEM((Z_ROWS, LANES), F32),
                VMEM((Z_ROWS, LANES), F32),
                pltpu.SemaphoreType.DMA((6,)),
            ],
            interpret=interpret,
            compiler_params=pltpu.CompilerParams(vmem_limit_bytes=4 << 20),
            name="pack_z",
        )(*(pltpu.with_memory_space_constraint(x, pltpu.HBM) for x in (source, occupancy, classes, screen_table, parents, coarse)))
        ha = swap(za, one)
        hb = swap(zb, two)
        fc = swap(rows, three)
        fd = swap(rows, four)
        xa, xb, start, mid, ghost, bricks = pl.pallas_call(
            extend_z,
            out_shape=(
                sds(X_ROWS, LANES), sds(X_ROWS, LANES), sds(64, LANES), sds(16, 16, LANES),
                sds(64, LANES), sds(64, LANES),
            ),
            in_specs=[vm, sm] + [vm] * 6,
            out_specs=(vm,) * 6,
            scratch_shapes=[
                VMEM((24, 512), F32),
                VMEM((256, 2 * LANES), F32),
                VMEM((Z_ROWS, LANES), F32),
                VMEM((Z_ROWS, LANES), F32),
                VMEM((X_ROWS, LANES), F32),
                VMEM((X_ROWS, LANES), F32),
            ],
            interpret=interpret,
            compiler_params=pltpu.CompilerParams(vmem_limit_bytes=8 << 20),
            name="extend_z",
        )(fine, parents, coarse, pown, ha, hb, fc, fd)
        ga = swap(xa, five)
        gb = swap(xb, six)
        return pl.pallas_call(
            sweep_all,
            out_shape=(sds(16, 16, 64), sds(CX, NY, CZ)),
            in_specs=[vm] * 7,
            out_specs=(hbm, hbm),
            scratch_shapes=[
                VMEM((26, 16, LANES), F32),
                VMEM((LANES, LANES), F32),
                VMEM((LANES, 3 * LANES), F32),
                VMEM((320, 2 * LANES), F32),
                VMEM((38, NY, LANES), F32),
                VMEM((38, NY, LANES), F32),
                VMEM((X_ROWS, LANES), F32),
                VMEM((X_ROWS, LANES), F32),
                VMEM((16, 16, 64), F32),
                VMEM((CX, NY, LANES), F32),
                pltpu.SemaphoreType.DMA((5,)),
            ],
            interpret=interpret,
            compiler_params=pltpu.CompilerParams(vmem_limit_bytes=16 << 20),
            name="sweep_all",
        )(fine, ga, gb, start, mid, ghost, bricks)

    return local


def solution(mesh, interpret=False):
    placed = (
        P("grp", None, "slab"),
        P("grp", None, "slab"),
        P("grp", None, "slab"),
        P(),
        P("grp", None, "slab"),
        P("grp", "slab", None),
    )
    return jax.shard_map(
        build(mesh, interpret),
        mesh=mesh,
        in_specs=placed,
        out_specs=(P("grp", None, "slab"), P("grp", None, "slab")),
        check_vma=False,
    )
```

time: 29.1 us -> 29.6 us (1.017)
  Pallas kernels: 10.3 us -> 11.2 us
    pallas_call x1, Pallas kernels: 7.38 us -> 8.44 us  [local(): pl.pallas_call(sweep_all, out_shape=(sds(16, 16, 64), sds(CX, NY, CZ)), i...]
where the time goes in v3:
time: 29.6 us; the launch traced here: 29.5 us
  Pallas kernels  11.2 us (38%)
  waiting for transfers between devices  8.98 us (30%)
  starting transfers between devices  8.68 us (29%)
  between operations  0.69 us (2%)
    ppermute x6, waiting for transfers between devices, swap(): return lax.ppermute(block, ('grp', 'slab'), pairs)  8.98 us
    ppermute x6, starting transfers between devices, swap(): return lax.ppermute(block, ('grp', 'slab'), pairs)  8.68 us
    pallas_call x1, Pallas kernels, local(): pl.pallas_call(sweep_all, out_shape=(sds(16, 16, 64), sds(CX, NY, CZ)), i...  8.44 us
    pallas_call x1, Pallas kernels, local(): pl.pallas_call(pack_z, out_shape=(sds(Z_ROWS, LANES), sds(Z_ROWS, LANES),...  1.47 us
    pallas_call x1, Pallas kernels, local(): pl.pallas_call(extend_z, out_shape=(sds(X_ROWS, LANES), sds(X_ROWS, LANES...  1.25 us
  transfers between devices with their start and end apart: 6, of which 4 were waited for; matrix products, arithmetic and copies ran while one was open for 0% of the time, Pallas kernels for 0%

profile of v3, /device:TPU:120, one launch (start us, length us, event | category | flops | bytes accessed | tf_op | source)
XLA Modules:
  0.0 29.5 jit_solution(18329139490279386548)
XLA Ops:
  0.6 0.0 copy-start.1
  0.6 1.5 %pack_z.1 = (f32[96,128]{1,0:T(8,128)S(1)}, f32[96,128]{1,0:T(8,128)S(1)}, f32[16,128]{1,0:T(8,128)S(1)}, f32[64,128]{1,0:T(8,128)S(1)}, f32[32,32,128]{2,1,0:T(8,128)S(1)}) custom-call(f32[32,32,128]{2,1,0:T(8,128)} %src_hbm.1, s32[4,4,16]{2,1,0:T(4,128)} %occ_hbm.1, s32[4,4,16]{2,1,0:T(4,128)} %cls_hbm.1, f32[16]{0:T(128)} %tab_hbm.1, s32[2,2,8]{2,1,0:T(2,128)} %par.1, ...), custom_call_target="tpu_custom_call" | custom-call | tf_op jit(solution)/shard_map/pack_z/pallas_call | solution.py:510
  2.1 0.0 copy-start
  2.1 0.1 collective-permute-start
  2.2 0.8 %collective-permute-start.1 = (f32[96,128]{1,0:T(8,128)S(1)}, f32[96,128]{1,0:T(8,128)S(1)}, u32[]{:S(2)}, u32[]{:S(2)}) collective-permute-start(f32[96,128]{1,0:T(8,128)S(1)} %get-tuple-element.16), channel_id=1, source_target_pairs={{0,32},{1,2},{2,1},{3,4},{4,3},{5,6},{6,5},{7,8},{8,7},{9,10},{10,... | collective-permute-start | bytes 147464 | tf_op jit(solution)/shard_map/ppermute | solution.py:508
  3.1 3.4 %collective-permute-start.3 = (f32[16,128]{1,0:T(8,128)S(1)}, f32[16,128]{1,0:T(8,128)S(1)}, u32[]{:S(2)}, u32[]{:S(2)}) collective-permute-start(f32[16,128]{1,0:T(8,128)S(1)} %get-tuple-element.17), channel_id=1, source_target_pairs={{0,1},{1,0},{2,4},{3,5},{4,2},{5,3},{6,8},{7,9},{8,6},{9,7},{10,12... | collective-permute-start | bytes 24584 | tf_op jit(solution)/shard_map/ppermute | solution.py:508
  6.5 0.0 collective-permute-start.2
  6.5 2.4 %collective-permute-done.3.fd = f32[16,128]{1,0:T(8,128)S(1)} collective-permute-done((f32[16,128]{1,0:T(8,128)S(1)}, f32[16,128]{1,0:T(8,128)S(1)}, u32[]{:S(2)}, u32[]{:S(2)}) %collective-permute-start.3) | collective-permute-done | bytes 8224 | tf_op jit(solution)/shard_map/ppermute | solution.py:508
  8.8 1.3 %collective-permute-done.2.fc = f32[16,128]{1,0:T(8,128)S(1)} collective-permute-done((f32[16,128]{1,0:T(8,128)S(1)}, f32[16,128]{1,0:T(8,128)S(1)}, u32[]{:S(2)}, u32[]{:S(2)}) %collective-permute-start.2) | collective-permute-done | bytes 8224 | tf_op jit(solution)/shard_map/ppermute | solution.py:508
  10.1 0.0 collective-permute-done.ha
  10.1 0.0 collective-permute-done.1.hb
  10.1 0.0 copy-done.1
  10.1 0.0 copy-done
  10.1 1.3 %extend_z.1 = (f32[168,128]{1,0:T(8,128)S(1)}, f32[168,128]{1,0:T(8,128)S(1)}, f32[64,128]{1,0:T(8,128)S(1)}, f32[16,16,128]{2,1,0:T(8,128)S(1)}, f32[64,128]{1,0:T(8,128)S(1)}, /*index=5*/f32[64,128]{1,0:T(8,128)S(1)}) custom-call(f32[32,32,128]{2,1,0:T(8,128)S(1)} %get-tuple-element.13.fine, s32[2,2,8]{2,1,0:T(2,128)S(1)} %copy-done.1, ...), custom_call_target="tpu_custom_call" | custom-call | tf_op jit(solution)/shard_map/extend_z/pallas_call | solution.py:536
  11.4 1.6 %collective-permute-start.4 = (f32[168,128]{1,0:T(8,128)S(1)}, f32[168,128]{1,0:T(8,128)S(1)}, u32[]{:S(2)}, u32[]{:S(2)}) collective-permute-start(f32[168,128]{1,0:T(8,128)S(1)} %get-tuple-element.18), channel_id=1, source_target_pairs={{0,32},{1,33},{2,34},{3,35},{4,36},{5,37},{6,38},{7,39},{8,40},{9,... | collective-permute-start | bytes 258056 | tf_op jit(solution)/shard_map/ppermute | solution.py:508
  13.0 2.8 %collective-permute-start.5 = (f32[168,128]{1,0:T(8,128)S(1)}, f32[168,128]{1,0:T(8,128)S(1)}, u32[]{:S(2)}, u32[]{:S(2)}) collective-permute-start(f32[168,128]{1,0:T(8,128)S(1)} %get-tuple-element.19), channel_id=1, source_target_pairs={{0,1},{1,0},{2,3},{3,2},{4,5},{5,4},{6,7},{7,6},{8,9},{9,8},{10,11... | collective-permute-start | bytes 258056 | tf_op jit(solution)/shard_map/ppermute | solution.py:508
  15.8 0.4 %collective-permute-done.4.xa = f32[168,128]{1,0:T(8,128)S(1)} collective-permute-done((f32[168,128]{1,0:T(8,128)S(1)}, f32[168,128]{1,0:T(8,128)S(1)}, u32[]{:S(2)}, u32[]{:S(2)}) %collective-permute-start.4) | collective-permute-done | bytes 86048 | tf_op jit(solution)/shard_map/ppermute | solution.py:508
  16.2 4.9 %collective-permute-done.5.xb = f32[168,128]{1,0:T(8,128)S(1)} collective-permute-done((f32[168,128]{1,0:T(8,128)S(1)}, f32[168,128]{1,0:T(8,128)S(1)}, u32[]{:S(2)}, u32[]{:S(2)}) %collective-permute-start.5) | collective-permute-done | bytes 86048 | tf_op jit(solution)/shard_map/ppermute | solution.py:508
  21.1 8.4 %sweep_all.1 = (f32[16,16,64]{2,1,0:T(8,128)}, f32[32,32,128]{2,1,0:T(8,128)}) custom-call(f32[32,32,128]{2,1,0:T(8,128)S(1)} %get-tuple-element.13.fine, f32[168,128]{1,0:T(8,128)S(1)} %collective-permute-done.4.xa, f32[168,128]{1,0:T(8,128)S(1)} %collective-permute-done.5.xb, f32[64,128]{1,0:T(8,128)S(1)} %get-tuple-element.20.start, ...), custom_call_target="tpu_custom_call" | custom-call | tf_op jit(solution)/shard_map/sweep_all/pallas_call | solution.py:558
Async XLA Ops:
  0.6 9.5 %copy-start.1 = (s32[2,2,8]{2,1,0:T(2,128)S(1)}, s32[2,2,8]{2,1,0:T(2,128)}, u32[]{:S(2)}) copy-start(s32[2,2,8]{2,1,0:T(2,128)} %par.1) | copy-start | bytes 388
  2.1 8.0 %copy-start = (f32[1,4,512]{2,1,0:T(4,128)S(1)}, f32[1,4,512]{2,1,0:T(4,128)}, u32[]{:S(2)}) copy-start(f32[1,4,512]{2,1,0:T(4,128)} %co.1) | copy-start | bytes 24580
  2.1 8.0 %collective-permute-start = (f32[96,128]{1,0:T(8,128)S(1)}, f32[96,128]{1,0:T(8,128)S(1)}, u32[]{:S(2)}, u32[]{:S(2)}) collective-permute-start(f32[96,128]{1,0:T(8,128)S(1)} %get-tuple-element.15), channel_id=1, source_target_pairs={{0,1},{1,0},{2,3},{3,2},{4,5},{5,4},{6,7},{7,6},{8,9},{9,8},{10,11... | collective-permute-start | bytes 147464 | tf_op jit(solution)/shard_map/ppermute | solution.py:508
  2.2 7.9 %collective-permute-start.1 = (f32[96,128]{1,0:T(8,128)S(1)}, f32[96,128]{1,0:T(8,128)S(1)}, u32[]{:S(2)}, u32[]{:S(2)}) collective-permute-start(f32[96,128]{1,0:T(8,128)S(1)} %get-tuple-element.16), channel_id=1, source_target_pairs={{0,32},{1,2},{2,1},{3,4},{4,3},{5,6},{6,5},{7,8},{8,7},{9,10},{10,... | collective-permute-start | bytes 147464 | tf_op jit(solution)/shard_map/ppermute | solution.py:508
  3.1 5.8 %collective-permute-start.3 = (f32[16,128]{1,0:T(8,128)S(1)}, f32[16,128]{1,0:T(8,128)S(1)}, u32[]{:S(2)}, u32[]{:S(2)}) collective-permute-start(f32[16,128]{1,0:T(8,128)S(1)} %get-tuple-element.17), channel_id=1, source_target_pairs={{0,1},{1,0},{2,4},{3,5},{4,2},{5,3},{6,8},{7,9},{8,6},{9,7},{10,12... | collective-permute-start | bytes 24584 | tf_op jit(solution)/shard_map/ppermute | solution.py:508
  6.5 3.7 %collective-permute-start.2 = (f32[16,128]{1,0:T(8,128)S(1)}, f32[16,128]{1,0:T(8,128)S(1)}, u32[]{:S(2)}, u32[]{:S(2)}) collective-permute-start(f32[16,128]{1,0:T(8,128)S(1)} %get-tuple-element.17), channel_id=1, source_target_pairs={{0,2},{1,3},{2,0},{3,1},{4,6},{5,7},{6,4},{7,5},{8,10},{9,11},{10,... | collective-permute-start | bytes 24584 | tf_op jit(solution)/shard_map/ppermute | solution.py:508
  11.4 4.8 %collective-permute-start.4 = (f32[168,128]{1,0:T(8,128)S(1)}, f32[168,128]{1,0:T(8,128)S(1)}, u32[]{:S(2)}, u32[]{:S(2)}) collective-permute-start(f32[168,128]{1,0:T(8,128)S(1)} %get-tuple-element.18), channel_id=1, source_target_pairs={{0,32},{1,33},{2,34},{3,35},{4,36},{5,37},{6,38},{7,39},{8,40},{9,... | collective-permute-start | bytes 258056 | tf_op jit(solution)/shard_map/ppermute | solution.py:508
  13.0 8.1 %collective-permute-start.5 = (f32[168,128]{1,0:T(8,128)S(1)}, f32[168,128]{1,0:T(8,128)S(1)}, u32[]{:S(2)}, u32[]{:S(2)}) collective-permute-start(f32[168,128]{1,0:T(8,128)S(1)} %get-tuple-element.19), channel_id=1, source_target_pairs={{0,1},{1,0},{2,3},{3,2},{4,5},{5,4},{6,7},{7,6},{8,9},{9,8},{10,11... | collective-permute-start | bytes 258056 | tf_op jit(solution)/shard_map/ppermute | solution.py:508

commit v4 on v3

--- a/solution.py
+++ b/solution.py
@@ -435,11 +435,15 @@
         low, high = -2 + n, 33 - n
         if n == 1:
             edges = [[zero] * 4 for _ in range(4)]
+            b, l = iota((LANES, LANES), 0), iota((LANES, LANES), 1)
+            hit = ((b == 127) & (l % 8 == 3)) | ((b == 0) & (l % 8 == 4))
+            wide = [source[x + 3] for x in range(low - 1, high + 2)]
+            wide = dot(jnp.concatenate(wide, axis=0), onehot(hit))
             for x in range(low - 1, high + 2):
                 g, i = x // 16 + 1, x % 16
                 for t in range(4):
-                    v = source[x + 3, 8 * t : 8 * t + 8, :]
-                    edges[g][t] = jnp.where(lane // 8 == i, turn(v, 8 * i + 4), edges[g][t])
+                    at = 32 * (x - low + 1) + 8 * t
+                    edges[g][t] = jnp.where(lane // 8 == i, wide[at : at + 8], edges[g][t])
         planes = {}
         for x in range(low - 1, high + 2):
             g, i = x // 16 + 1, x % 16

time: 29.6 us -> 25.5 us (0.86)
  Pallas kernels: 11.2 us -> 7.07 us
    pallas_call x1, Pallas kernels: 8.44 us -> 4.35 us  [local(): pl.pallas_call(sweep_all, out_shape=(sds(16, 16, 64), sds(CX, NY, CZ)), i...]
where the time goes in v4:
time: 25.5 us; the launch traced here: 25.4 us
  waiting for transfers between devices  8.98 us (35%)
  starting transfers between devices  8.68 us (34%)
  Pallas kernels  7.07 us (28%)
  between operations  0.69 us (3%)
    ppermute x6, waiting for transfers between devices, swap(): return lax.ppermute(block, ('grp', 'slab'), pairs)  8.98 us
    ppermute x6, starting transfers between devices, swap(): return lax.ppermute(block, ('grp', 'slab'), pairs)  8.68 us
    pallas_call x1, Pallas kernels, local(): pl.pallas_call(sweep_all, out_shape=(sds(16, 16, 64), sds(CX, NY, CZ)), i...  4.35 us
    pallas_call x1, Pallas kernels, local(): pl.pallas_call(pack_z, out_shape=(sds(Z_ROWS, LANES), sds(Z_ROWS, LANES),...  1.47 us
    pallas_call x1, Pallas kernels, local(): pl.pallas_call(extend_z, out_shape=(sds(X_ROWS, LANES), sds(X_ROWS, LANES...  1.25 us
  transfers between devices with their start and end apart: 6, of which 4 were waited for; matrix products, arithmetic and copies ran while one was open for 0% of the time, Pallas kernels for 0%

profile of v4, /device:TPU:120, one launch (start us, length us, event | category | flops | bytes accessed | tf_op | source)
XLA Modules:
  0.0 25.4 jit_solution(6892845020764285070)
XLA Ops:
  0.6 0.0 copy-start.1
  0.6 1.5 %pack_z.1 = (f32[96,128]{1,0:T(8,128)S(1)}, f32[96,128]{1,0:T(8,128)S(1)}, f32[16,128]{1,0:T(8,128)S(1)}, f32[64,128]{1,0:T(8,128)S(1)}, f32[32,32,128]{2,1,0:T(8,128)S(1)}) custom-call(f32[32,32,128]{2,1,0:T(8,128)} %src_hbm.1, s32[4,4,16]{2,1,0:T(4,128)} %occ_hbm.1, s32[4,4,16]{2,1,0:T(4,128)} %cls_hbm.1, f32[16]{0:T(128)} %tab_hbm.1, s32[2,2,8]{2,1,0:T(2,128)} %par.1, ...), custom_call_target="tpu_custom_call" | custom-call | tf_op jit(solution)/shard_map/pack_z/pallas_call | solution.py:514
  2.1 0.0 copy-start
  2.1 0.1 collective-permute-start
  2.2 0.8 %collective-permute-start.1 = (f32[96,128]{1,0:T(8,128)S(1)}, f32[96,128]{1,0:T(8,128)S(1)}, u32[]{:S(2)}, u32[]{:S(2)}) collective-permute-start(f32[96,128]{1,0:T(8,128)S(1)} %get-tuple-element.16), channel_id=1, source_target_pairs={{0,32},{1,2},{2,1},{3,4},{4,3},{5,6},{6,5},{7,8},{8,7},{9,10},{10,... | collective-permute-start | bytes 147464 | tf_op jit(solution)/shard_map/ppermute | solution.py:512
  3.1 3.4 %collective-permute-start.3 = (f32[16,128]{1,0:T(8,128)S(1)}, f32[16,128]{1,0:T(8,128)S(1)}, u32[]{:S(2)}, u32[]{:S(2)}) collective-permute-start(f32[16,128]{1,0:T(8,128)S(1)} %get-tuple-element.17), channel_id=1, source_target_pairs={{0,1},{1,0},{2,4},{3,5},{4,2},{5,3},{6,8},{7,9},{8,6},{9,7},{10,12... | collective-permute-start | bytes 24584 | tf_op jit(solution)/shard_map/ppermute | solution.py:512
  6.5 0.0 collective-permute-start.2
  6.5 2.4 %collective-permute-done.3.fd = f32[16,128]{1,0:T(8,128)S(1)} collective-permute-done((f32[16,128]{1,0:T(8,128)S(1)}, f32[16,128]{1,0:T(8,128)S(1)}, u32[]{:S(2)}, u32[]{:S(2)}) %collective-permute-start.3) | collective-permute-done | bytes 8224 | tf_op jit(solution)/shard_map/ppermute | solution.py:512
  8.8 1.3 %collective-permute-done.2.fc = f32[16,128]{1,0:T(8,128)S(1)} collective-permute-done((f32[16,128]{1,0:T(8,128)S(1)}, f32[16,128]{1,0:T(8,128)S(1)}, u32[]{:S(2)}, u32[]{:S(2)}) %collective-permute-start.2) | collective-permute-done | bytes 8224 | tf_op jit(solution)/shard_map/ppermute | solution.py:512
  10.1 0.0 collective-permute-done.ha
  10.1 0.0 collective-permute-done.1.hb
  10.1 0.0 copy-done.1
  10.1 0.0 copy-done
  10.1 1.3 %extend_z.1 = (f32[168,128]{1,0:T(8,128)S(1)}, f32[168,128]{1,0:T(8,128)S(1)}, f32[64,128]{1,0:T(8,128)S(1)}, f32[16,16,128]{2,1,0:T(8,128)S(1)}, f32[64,128]{1,0:T(8,128)S(1)}, /*index=5*/f32[64,128]{1,0:T(8,128)S(1)}) custom-call(f32[32,32,128]{2,1,0:T(8,128)S(1)} %get-tuple-element.13.fine, s32[2,2,8]{2,1,0:T(2,128)S(1)} %copy-done.1, ...), custom_call_target="tpu_custom_call" | custom-call | tf_op jit(solution)/shard_map/extend_z/pallas_call | solution.py:540
  11.4 1.6 %collective-permute-start.4 = (f32[168,128]{1,0:T(8,128)S(1)}, f32[168,128]{1,0:T(8,128)S(1)}, u32[]{:S(2)}, u32[]{:S(2)}) collective-permute-start(f32[168,128]{1,0:T(8,128)S(1)} %get-tuple-element.18), channel_id=1, source_target_pairs={{0,32},{1,33},{2,34},{3,35},{4,36},{5,37},{6,38},{7,39},{8,40},{9,... | collective-permute-start | bytes 258056 | tf_op jit(solution)/shard_map/ppermute | solution.py:512
  13.0 2.8 %collective-permute-start.5 = (f32[168,128]{1,0:T(8,128)S(1)}, f32[168,128]{1,0:T(8,128)S(1)}, u32[]{:S(2)}, u32[]{:S(2)}) collective-permute-start(f32[168,128]{1,0:T(8,128)S(1)} %get-tuple-element.19), channel_id=1, source_target_pairs={{0,1},{1,0},{2,3},{3,2},{4,5},{5,4},{6,7},{7,6},{8,9},{9,8},{10,11... | collective-permute-start | bytes 258056 | tf_op jit(solution)/shard_map/ppermute | solution.py:512
  15.8 0.4 %collective-permute-done.4.xa = f32[168,128]{1,0:T(8,128)S(1)} collective-permute-done((f32[168,128]{1,0:T(8,128)S(1)}, f32[168,128]{1,0:T(8,128)S(1)}, u32[]{:S(2)}, u32[]{:S(2)}) %collective-permute-start.4) | collective-permute-done | bytes 86048 | tf_op jit(solution)/shard_map/ppermute | solution.py:512
  16.2 4.9 %collective-permute-done.5.xb = f32[168,128]{1,0:T(8,128)S(1)} collective-permute-done((f32[168,128]{1,0:T(8,128)S(1)}, f32[168,128]{1,0:T(8,128)S(1)}, u32[]{:S(2)}, u32[]{:S(2)}) %collective-permute-start.5) | collective-permute-done | bytes 86048 | tf_op jit(solution)/shard_map/ppermute | solution.py:512
  21.1 4.3 %sweep_all.1 = (f32[16,16,64]{2,1,0:T(8,128)}, f32[32,32,128]{2,1,0:T(8,128)}) custom-call(f32[32,32,128]{2,1,0:T(8,128)S(1)} %get-tuple-element.13.fine, f32[168,128]{1,0:T(8,128)S(1)} %collective-permute-done.4.xa, f32[168,128]{1,0:T(8,128)S(1)} %collective-permute-done.5.xb, f32[64,128]{1,0:T(8,128)S(1)} %get-tuple-element.20.start, ...), custom_call_target="tpu_custom_call" | custom-call | tf_op jit(solution)/shard_map/sweep_all/pallas_call | solution.py:562
Async XLA Ops:
  0.6 9.5 %copy-start.1 = (s32[2,2,8]{2,1,0:T(2,128)S(1)}, s32[2,2,8]{2,1,0:T(2,128)}, u32[]{:S(2)}) copy-start(s32[2,2,8]{2,1,0:T(2,128)} %par.1) | copy-start | bytes 388
  2.1 8.0 %copy-start = (f32[1,4,512]{2,1,0:T(4,128)S(1)}, f32[1,4,512]{2,1,0:T(4,128)}, u32[]{:S(2)}) copy-start(f32[1,4,512]{2,1,0:T(4,128)} %co.1) | copy-start | bytes 24580
  2.1 8.0 %collective-permute-start = (f32[96,128]{1,0:T(8,128)S(1)}, f32[96,128]{1,0:T(8,128)S(1)}, u32[]{:S(2)}, u32[]{:S(2)}) collective-permute-start(f32[96,128]{1,0:T(8,128)S(1)} %get-tuple-element.15), channel_id=1, source_target_pairs={{0,1},{1,0},{2,3},{3,2},{4,5},{5,4},{6,7},{7,6},{8,9},{9,8},{10,11... | collective-permute-start | bytes 147464 | tf_op jit(solution)/shard_map/ppermute | solution.py:512
  2.2 7.9 %collective-permute-start.1 = (f32[96,128]{1,0:T(8,128)S(1)}, f32[96,128]{1,0:T(8,128)S(1)}, u32[]{:S(2)}, u32[]{:S(2)}) collective-permute-start(f32[96,128]{1,0:T(8,128)S(1)} %get-tuple-element.16), channel_id=1, source_target_pairs={{0,32},{1,2},{2,1},{3,4},{4,3},{5,6},{6,5},{7,8},{8,7},{9,10},{10,... | collective-permute-start | bytes 147464 | tf_op jit(solution)/shard_map/ppermute | solution.py:512
  3.1 5.8 %collective-permute-start.3 = (f32[16,128]{1,0:T(8,128)S(1)}, f32[16,128]{1,0:T(8,128)S(1)}, u32[]{:S(2)}, u32[]{:S(2)}) collective-permute-start(f32[16,128]{1,0:T(8,128)S(1)} %get-tuple-element.17), channel_id=1, source_target_pairs={{0,1},{1,0},{2,4},{3,5},{4,2},{5,3},{6,8},{7,9},{8,6},{9,7},{10,12... | collective-permute-start | bytes 24584 | tf_op jit(solution)/shard_map/ppermute | solution.py:512
  6.5 3.7 %collective-permute-start.2 = (f32[16,128]{1,0:T(8,128)S(1)}, f32[16,128]{1,0:T(8,128)S(1)}, u32[]{:S(2)}, u32[]{:S(2)}) collective-permute-start(f32[16,128]{1,0:T(8,128)S(1)} %get-tuple-element.17), channel_id=1, source_target_pairs={{0,2},{1,3},{2,0},{3,1},{4,6},{5,7},{6,4},{7,5},{8,10},{9,11},{10,... | collective-permute-start | bytes 24584 | tf_op jit(solution)/shard_map/ppermute | solution.py:512
  11.4 4.8 %collective-permute-start.4 = (f32[168,128]{1,0:T(8,128)S(1)}, f32[168,128]{1,0:T(8,128)S(1)}, u32[]{:S(2)}, u32[]{:S(2)}) collective-permute-start(f32[168,128]{1,0:T(8,128)S(1)} %get-tuple-element.18), channel_id=1, source_target_pairs={{0,32},{1,33},{2,34},{3,35},{4,36},{5,37},{6,38},{7,39},{8,40},{9,... | collective-permute-start | bytes 258056 | tf_op jit(solution)/shard_map/ppermute | solution.py:512
  13.0 8.1 %collective-permute-start.5 = (f32[168,128]{1,0:T(8,128)S(1)}, f32[168,128]{1,0:T(8,128)S(1)}, u32[]{:S(2)}, u32[]{:S(2)}) collective-permute-start(f32[168,128]{1,0:T(8,128)S(1)} %get-tuple-element.19), channel_id=1, source_target_pairs={{0,1},{1,0},{2,3},{3,2},{4,5},{5,4},{6,7},{7,6},{8,9},{9,8},{10,11... | collective-permute-start | bytes 258056 | tf_op jit(solution)/shard_map/ppermute | solution.py:512

commit v5 on v4

--- a/solution.py
+++ b/solution.py
@@ -5,7 +5,6 @@
 from jax.experimental.pallas import tpu as pltpu
 from jax.sharding import PartitionSpec as P
 
-BRICK = 8
 SWEEPS = 3
 
 screen_strength = 4.0
@@ -326,10 +325,11 @@
     mid_copy = pltpu.make_async_copy(mid_out, mid_hbm, sems.at[0])
     mid_copy.start()
 
-    b, l = iota((LANES, 2 * LANES), 0), iota((LANES, 2 * LANES), 1)
+    b, l = iota((LANES, 3 * LANES), 0), iota((LANES, 3 * LANES), 1)
     j = l % 8
     hit = (l < 128) & (b == l // 2)
-    hit = hit | ((l >= 128) & (b == jnp.where(j < 4, 126 + j // 2, 62 + j // 2)))
+    hit = hit | ((l >= 128) & (l < 256) & (b == jnp.where(j < 4, 126 + j // 2, 62 + j // 2)))
+    hit = hit | ((l >= 256) & (b == jnp.where(j < 4, 63, 0)))
     parents = jnp.concatenate(
         [
             jnp.where(inverse13(x // 4) != 0.0, v13[x + 5, 8 * u : 8 * u + 8, :], 0.0)
@@ -348,7 +348,7 @@
     for q in range(-2, 18):
         g, i = q // 8 + 1, q % 8
         for u in range(2):
-            v = rep[16 * (q + 2) + 8 * u : 16 * (q + 2) + 8 * u + 8, LANES:]
+            v = rep[16 * (q + 2) + 8 * u : 16 * (q + 2) + 8 * u + 8, LANES : 2 * LANES]
             halo[g][u] = jnp.where(lane // 16 == i, v, halo[g][u])
     halo = [[tiles[t // 2] for t in range(4)] for tiles in halo]
     halo_rhs, halo_inverse, halo_weight = [], [], []
@@ -406,10 +406,10 @@
 
     edges = [[zero, zero] for _ in range(4)]
     for q in range(-2, 18):
-        for child in range(2):
-            g, i = (2 * q) // 16 + 1, (2 * q) % 16 + child
-            for u in range(2):
-                edges[g][u] = jnp.where(lane // 8 == i, turn(parent(q, u), 8 * i + 4), edges[g][u])
+        g, i = q // 8 + 1, q % 8
+        for u in range(2):
+            v = rep[16 * (q + 2) + 8 * u : 16 * (q + 2) + 8 * u + 8, 2 * LANES :]
+            edges[g][u] = jnp.where(lane // 16 == i, v, edges[g][u])
     edges = [[tiles[t // 2] for t in range(4)] for tiles in edges]
     planes = {}
     for q in range(-2, 18):
@@ -568,7 +568,7 @@
                 VMEM((26, 16, LANES), F32),
                 VMEM((LANES, LANES), F32),
                 VMEM((LANES, 3 * LANES), F32),
-                VMEM((320, 2 * LANES), F32),
+                VMEM((320, 3 * LANES), F32),
                 VMEM((38, NY, LANES), F32),
                 VMEM((38, NY, LANES), F32),
                 VMEM((X_ROWS, LANES), F32),

time: 25.5 us -> 25.4 us (level)
  no operation moved by 1% of the time
where the time goes in v5:
time: 25.4 us; the launch traced here: 25.3 us
  waiting for transfers between devices  8.98 us (35%)
  starting transfers between devices  8.68 us (34%)
  Pallas kernels  6.98 us (27%)
  between operations  0.69 us (3%)
    ppermute x6, waiting for transfers between devices, swap(): return lax.ppermute(block, ('grp', 'slab'), pairs)  8.98 us
    ppermute x6, starting transfers between devices, swap(): return lax.ppermute(block, ('grp', 'slab'), pairs)  8.68 us
    pallas_call x1, Pallas kernels, local(): pl.pallas_call(sweep_all, out_shape=(sds(16, 16, 64), sds(CX, NY, CZ)), i...  4.25 us
    pallas_call x1, Pallas kernels, local(): pl.pallas_call(pack_z, out_shape=(sds(Z_ROWS, LANES), sds(Z_ROWS, LANES),...  1.47 us
    pallas_call x1, Pallas kernels, local(): pl.pallas_call(extend_z, out_shape=(sds(X_ROWS, LANES), sds(X_ROWS, LANES...  1.25 us
  transfers between devices with their start and end apart: 6, of which 4 were waited for; matrix products, arithmetic and copies ran while one was open for 0% of the time, Pallas kernels for 0%

profile of v5, /device:TPU:120, one launch (start us, length us, event | category | flops | bytes accessed | tf_op | source)
XLA Modules:
  0.0 25.3 jit_solution(10127542709101474573)
XLA Ops:
  0.6 0.0 copy-start.1
  0.6 1.5 %pack_z.1 = (f32[96,128]{1,0:T(8,128)S(1)}, f32[96,128]{1,0:T(8,128)S(1)}, f32[16,128]{1,0:T(8,128)S(1)}, f32[64,128]{1,0:T(8,128)S(1)}, f32[32,32,128]{2,1,0:T(8,128)S(1)}) custom-call(f32[32,32,128]{2,1,0:T(8,128)} %src_hbm.1, s32[4,4,16]{2,1,0:T(4,128)} %occ_hbm.1, s32[4,4,16]{2,1,0:T(4,128)} %cls_hbm.1, f32[16]{0:T(128)} %tab_hbm.1, s32[2,2,8]{2,1,0:T(2,128)} %par.1, ...), custom_call_target="tpu_custom_call" | custom-call | tf_op jit(solution)/shard_map/pack_z/pallas_call | solution.py:514
  2.1 0.0 copy-start
  2.1 0.1 collective-permute-start
  2.2 0.8 %collective-permute-start.1 = (f32[96,128]{1,0:T(8,128)S(1)}, f32[96,128]{1,0:T(8,128)S(1)}, u32[]{:S(2)}, u32[]{:S(2)}) collective-permute-start(f32[96,128]{1,0:T(8,128)S(1)} %get-tuple-element.16), channel_id=1, source_target_pairs={{0,32},{1,2},{2,1},{3,4},{4,3},{5,6},{6,5},{7,8},{8,7},{9,10},{10,... | collective-permute-start | bytes 147464 | tf_op jit(solution)/shard_map/ppermute | solution.py:512
  3.1 3.4 %collective-permute-start.3 = (f32[16,128]{1,0:T(8,128)S(1)}, f32[16,128]{1,0:T(8,128)S(1)}, u32[]{:S(2)}, u32[]{:S(2)}) collective-permute-start(f32[16,128]{1,0:T(8,128)S(1)} %get-tuple-element.17), channel_id=1, source_target_pairs={{0,1},{1,0},{2,4},{3,5},{4,2},{5,3},{6,8},{7,9},{8,6},{9,7},{10,12... | collective-permute-start | bytes 24584 | tf_op jit(solution)/shard_map/ppermute | solution.py:512
  6.5 0.0 collective-permute-start.2
  6.5 2.4 %collective-permute-done.3.fd = f32[16,128]{1,0:T(8,128)S(1)} collective-permute-done((f32[16,128]{1,0:T(8,128)S(1)}, f32[16,128]{1,0:T(8,128)S(1)}, u32[]{:S(2)}, u32[]{:S(2)}) %collective-permute-start.3) | collective-permute-done | bytes 8224 | tf_op jit(solution)/shard_map/ppermute | solution.py:512
  8.8 1.3 %collective-permute-done.2.fc = f32[16,128]{1,0:T(8,128)S(1)} collective-permute-done((f32[16,128]{1,0:T(8,128)S(1)}, f32[16,128]{1,0:T(8,128)S(1)}, u32[]{:S(2)}, u32[]{:S(2)}) %collective-permute-start.2) | collective-permute-done | bytes 8224 | tf_op jit(solution)/shard_map/ppermute | solution.py:512
  10.1 0.0 collective-permute-done.ha
  10.1 0.0 collective-permute-done.1.hb
  10.1 0.0 copy-done.1
  10.1 0.0 copy-done
  10.1 1.3 %extend_z.1 = (f32[168,128]{1,0:T(8,128)S(1)}, f32[168,128]{1,0:T(8,128)S(1)}, f32[64,128]{1,0:T(8,128)S(1)}, f32[16,16,128]{2,1,0:T(8,128)S(1)}, f32[64,128]{1,0:T(8,128)S(1)}, /*index=5*/f32[64,128]{1,0:T(8,128)S(1)}) custom-call(f32[32,32,128]{2,1,0:T(8,128)S(1)} %get-tuple-element.13.fine, s32[2,2,8]{2,1,0:T(2,128)S(1)} %copy-done.1, ...), custom_call_target="tpu_custom_call" | custom-call | tf_op jit(solution)/shard_map/extend_z/pallas_call | solution.py:540
  11.4 1.6 %collective-permute-start.4 = (f32[168,128]{1,0:T(8,128)S(1)}, f32[168,128]{1,0:T(8,128)S(1)}, u32[]{:S(2)}, u32[]{:S(2)}) collective-permute-start(f32[168,128]{1,0:T(8,128)S(1)} %get-tuple-element.18), channel_id=1, source_target_pairs={{0,32},{1,33},{2,34},{3,35},{4,36},{5,37},{6,38},{7,39},{8,40},{9,... | collective-permute-start | bytes 258056 | tf_op jit(solution)/shard_map/ppermute | solution.py:512
  13.0 2.8 %collective-permute-start.5 = (f32[168,128]{1,0:T(8,128)S(1)}, f32[168,128]{1,0:T(8,128)S(1)}, u32[]{:S(2)}, u32[]{:S(2)}) collective-permute-start(f32[168,128]{1,0:T(8,128)S(1)} %get-tuple-element.19), channel_id=1, source_target_pairs={{0,1},{1,0},{2,3},{3,2},{4,5},{5,4},{6,7},{7,6},{8,9},{9,8},{10,11... | collective-permute-start | bytes 258056 | tf_op jit(solution)/shard_map/ppermute | solution.py:512
  15.8 0.4 %collective-permute-done.4.xa = f32[168,128]{1,0:T(8,128)S(1)} collective-permute-done((f32[168,128]{1,0:T(8,128)S(1)}, f32[168,128]{1,0:T(8,128)S(1)}, u32[]{:S(2)}, u32[]{:S(2)}) %collective-permute-start.4) | collective-permute-done | bytes 86048 | tf_op jit(solution)/shard_map/ppermute | solution.py:512
  16.2 4.9 %collective-permute-done.5.xb = f32[168,128]{1,0:T(8,128)S(1)} collective-permute-done((f32[168,128]{1,0:T(8,128)S(1)}, f32[168,128]{1,0:T(8,128)S(1)}, u32[]{:S(2)}, u32[]{:S(2)}) %collective-permute-start.5) | collective-permute-done | bytes 86048 | tf_op jit(solution)/shard_map/ppermute | solution.py:512
  21.1 4.2 %sweep_all.1 = (f32[16,16,64]{2,1,0:T(8,128)}, f32[32,32,128]{2,1,0:T(8,128)}) custom-call(f32[32,32,128]{2,1,0:T(8,128)S(1)} %get-tuple-element.13.fine, f32[168,128]{1,0:T(8,128)S(1)} %collective-permute-done.4.xa, f32[168,128]{1,0:T(8,128)S(1)} %collective-permute-done.5.xb, f32[64,128]{1,0:T(8,128)S(1)} %get-tuple-element.20.start, ...), custom_call_target="tpu_custom_call" | custom-call | tf_op jit(solution)/shard_map/sweep_all/pallas_call | solution.py:562
Async XLA Ops:
  0.6 9.5 %copy-start.1 = (s32[2,2,8]{2,1,0:T(2,128)S(1)}, s32[2,2,8]{2,1,0:T(2,128)}, u32[]{:S(2)}) copy-start(s32[2,2,8]{2,1,0:T(2,128)} %par.1) | copy-start | bytes 388
  2.1 8.0 %copy-start = (f32[1,4,512]{2,1,0:T(4,128)S(1)}, f32[1,4,512]{2,1,0:T(4,128)}, u32[]{:S(2)}) copy-start(f32[1,4,512]{2,1,0:T(4,128)} %co.1) | copy-start | bytes 24580
  2.1 8.0 %collective-permute-start = (f32[96,128]{1,0:T(8,128)S(1)}, f32[96,128]{1,0:T(8,128)S(1)}, u32[]{:S(2)}, u32[]{:S(2)}) collective-permute-start(f32[96,128]{1,0:T(8,128)S(1)} %get-tuple-element.15), channel_id=1, source_target_pairs={{0,1},{1,0},{2,3},{3,2},{4,5},{5,4},{6,7},{7,6},{8,9},{9,8},{10,11... | collective-permute-start | bytes 147464 | tf_op jit(solution)/shard_map/ppermute | solution.py:512
  2.2 7.9 %collective-permute-start.1 = (f32[96,128]{1,0:T(8,128)S(1)}, f32[96,128]{1,0:T(8,128)S(1)}, u32[]{:S(2)}, u32[]{:S(2)}) collective-permute-start(f32[96,128]{1,0:T(8,128)S(1)} %get-tuple-element.16), channel_id=1, source_target_pairs={{0,32},{1,2},{2,1},{3,4},{4,3},{5,6},{6,5},{7,8},{8,7},{9,10},{10,... | collective-permute-start | bytes 147464 | tf_op jit(solution)/shard_map/ppermute | solution.py:512
  3.1 5.8 %collective-permute-start.3 = (f32[16,128]{1,0:T(8,128)S(1)}, f32[16,128]{1,0:T(8,128)S(1)}, u32[]{:S(2)}, u32[]{:S(2)}) collective-permute-start(f32[16,128]{1,0:T(8,128)S(1)} %get-tuple-element.17), channel_id=1, source_target_pairs={{0,1},{1,0},{2,4},{3,5},{4,2},{5,3},{6,8},{7,9},{8,6},{9,7},{10,12... | collective-permute-start | bytes 24584 | tf_op jit(solution)/shard_map/ppermute | solution.py:512
  6.5 3.7 %collective-permute-start.2 = (f32[16,128]{1,0:T(8,128)S(1)}, f32[16,128]{1,0:T(8,128)S(1)}, u32[]{:S(2)}, u32[]{:S(2)}) collective-permute-start(f32[16,128]{1,0:T(8,128)S(1)} %get-tuple-element.17), channel_id=1, source_target_pairs={{0,2},{1,3},{2,0},{3,1},{4,6},{5,7},{6,4},{7,5},{8,10},{9,11},{10,... | collective-permute-start | bytes 24584 | tf_op jit(solution)/shard_map/ppermute | solution.py:512
  11.4 4.8 %collective-permute-start.4 = (f32[168,128]{1,0:T(8,128)S(1)}, f32[168,128]{1,0:T(8,128)S(1)}, u32[]{:S(2)}, u32[]{:S(2)}) collective-permute-start(f32[168,128]{1,0:T(8,128)S(1)} %get-tuple-element.18), channel_id=1, source_target_pairs={{0,32},{1,33},{2,34},{3,35},{4,36},{5,37},{6,38},{7,39},{8,40},{9,... | collective-permute-start | bytes 258056 | tf_op jit(solution)/shard_map/ppermute | solution.py:512
  13.0 8.1 %collective-permute-start.5 = (f32[168,128]{1,0:T(8,128)S(1)}, f32[168,128]{1,0:T(8,128)S(1)}, u32[]{:S(2)}, u32[]{:S(2)}) collective-permute-start(f32[168,128]{1,0:T(8,128)S(1)} %get-tuple-element.19), channel_id=1, source_target_pairs={{0,1},{1,0},{2,3},{3,2},{4,5},{5,4},{6,7},{7,6},{8,9},{9,8},{10,11... | collective-permute-start | bytes 258056 | tf_op jit(solution)/shard_map/ppermute | solution.py:512

commit v6 on v5

--- a/solution.py
+++ b/solution.py
@@ -22,7 +22,7 @@
 COARSE = 4
 
 Z_COARSE, Z_POS, Z_BRICK, Z_SRC, Z_ROWS = 0, 16, 24, 32, 96
-X_START, X_MID, X_FINE, X_GHOST, X_BRICK, X_ROWS = 0, 24, 88, 152, 160, 168
+X_START, X_MID, X_FINE, X_GHOST, X_BRICK, X_ROWS = 0, 24, 64, 128, 136, 144
 
 
 def iota(shape, dim):
@@ -220,8 +220,16 @@
         mid[i] = summed[16 * i : 16 * (i + 1)]
     for out, rows, m0, f0, g0, b0, edge in ((xl, 0, 0, 0, 0, 0, 0), (xr, 40, 12, 30, 1, 2, 16)):
         out[X_START : X_START + 24, :] = start[rows : rows + 24, :]
+        sides = jnp.zeros((8, LANES), F32)
         for i in range(4):
-            out[X_MID + 16 * i : X_MID + 16 * (i + 1), :] = mid[m0 + i]
+            for u in range(2):
+                v = mid[m0 + i, 8 * u : 8 * u + 8, :]
+                sides = jnp.where(lane % 64 // 8 == 2 * i + u, turn(v, 4 + 8 * (2 * i + u)), sides)
+                if i % 2 == 0:
+                    at = X_MID + 8 * i + 8 * u
+                    other = turn(mid[m0 + i + 1, 8 * u : 8 * u + 8, :], 64)
+                    out[at : at + 8, :] = jnp.where(lane < 64, v, other)
+        out[X_MID + 32 : X_MID + 40, :] = sides
         for i in range(2):
             out[X_FINE + NY * i : X_FINE + NY * (i + 1), :] = fine[f0 + i]
         packed = jnp.zeros((8, LANES), F32)
@@ -240,7 +248,7 @@
 
 def sweep_all(
     fine, xa, xb, start, smid, sghost, bricks, mid_hbm, fin_hbm,
-    v13, pext, coef, rep, m1, m2, xl, xr, mid_out, fin_out, sems,
+    v13, pext, coef, rep, m1, m2, xl, xr, mid_out, fin_out, xm, sems,
 ):
     grp = lax.axis_index("grp")
     even = grp % 2 == 0
@@ -297,11 +305,19 @@
         v13[x + 5, 0:8, :] = v
         v13[x + 5, 8:16, :] = v
 
+    for base, edge in ((0, xl), (4, xr)):
+        sides = edge[X_MID + 32 : X_MID + 40, :]
+        for i in range(4):
+            for u in range(2):
+                at = X_MID + 16 * (i // 2) + 8 * u
+                v = turn(edge[at : at + 8, :], 64 * (i % 2))
+                xm[base + i, 8 * u : 8 * u + 8, :] = jnp.where(lane < 64, v, turn(sides, -(4 + 8 * (2 * i + u))))
+
     def rhs13(x, u):
         if x < 0:
-            return xl[X_MID + 16 * (x + 4) + 8 * u : X_MID + 16 * (x + 4) + 8 * u + 8, :]
+            return xm[x + 4, 8 * u : 8 * u + 8, :]
         if x > 15:
-            return xr[X_MID + 16 * (x - 16) + 8 * u : X_MID + 16 * (x - 16) + 8 * u + 8, :]
+            return xm[x - 12, 8 * u : 8 * u + 8, :]
         return smid[x, 8 * u : 8 * u + 8, :]
 
     for n in range(SWEEPS):
@@ -575,6 +591,7 @@
                 VMEM((X_ROWS, LANES), F32),
                 VMEM((16, 16, 64), F32),
                 VMEM((CX, NY, LANES), F32),
+                VMEM((8, 16, LANES), F32),
                 pltpu.SemaphoreType.DMA((5,)),
             ],
             interpret=interpret,

time: 25.4 us -> 25.3 us (level)
  no operation moved by 1% of the time
where the time goes in v6:
time: 25.3 us; the launch traced here: 25.2 us
  waiting for transfers between devices  8.85 us (35%)
  starting transfers between devices  8.68 us (34%)
  Pallas kernels  7 us (28%)
  between operations  0.69 us (3%)
    ppermute x6, waiting for transfers between devices, swap(): return lax.ppermute(block, ('grp', 'slab'), pairs)  8.85 us
    ppermute x6, starting transfers between devices, swap(): return lax.ppermute(block, ('grp', 'slab'), pairs)  8.68 us
    pallas_call x1, Pallas kernels, local(): pl.pallas_call(sweep_all, out_shape=(sds(16, 16, 64), sds(CX, NY, CZ)), i...  4.2 us
    pallas_call x1, Pallas kernels, local(): pl.pallas_call(pack_z, out_shape=(sds(Z_ROWS, LANES), sds(Z_ROWS, LANES),...  1.47 us
    pallas_call x1, Pallas kernels, local(): pl.pallas_call(extend_z, out_shape=(sds(X_ROWS, LANES), sds(X_ROWS, LANES...  1.33 us
  transfers between devices with their start and end apart: 6, of which 4 were waited for; matrix products, arithmetic and copies ran while one was open for 0% of the time, Pallas kernels for 0%

profile of v6, /device:TPU:120, one launch (start us, length us, event | category | flops | bytes accessed | tf_op | source)
XLA Modules:
  0.0 25.2 jit_solution(5099530627505854936)
XLA Ops:
  0.6 0.0 copy-start.1
  0.6 1.5 %pack_z.1 = (f32[96,128]{1,0:T(8,128)S(1)}, f32[96,128]{1,0:T(8,128)S(1)}, f32[16,128]{1,0:T(8,128)S(1)}, f32[64,128]{1,0:T(8,128)S(1)}, f32[32,32,128]{2,1,0:T(8,128)S(1)}) custom-call(f32[32,32,128]{2,1,0:T(8,128)} %src_hbm.1, s32[4,4,16]{2,1,0:T(4,128)} %occ_hbm.1, s32[4,4,16]{2,1,0:T(4,128)} %cls_hbm.1, f32[16]{0:T(128)} %tab_hbm.1, s32[2,2,8]{2,1,0:T(2,128)} %par.1, ...), custom_call_target="tpu_custom_call" | custom-call | tf_op jit(solution)/shard_map/pack_z/pallas_call | solution.py:530
  2.1 0.0 copy-start
  2.1 0.1 collective-permute-start
  2.2 0.8 %collective-permute-start.1 = (f32[96,128]{1,0:T(8,128)S(1)}, f32[96,128]{1,0:T(8,128)S(1)}, u32[]{:S(2)}, u32[]{:S(2)}) collective-permute-start(f32[96,128]{1,0:T(8,128)S(1)} %get-tuple-element.16), channel_id=1, source_target_pairs={{0,32},{1,2},{2,1},{3,4},{4,3},{5,6},{6,5},{7,8},{8,7},{9,10},{10,... | collective-permute-start | bytes 147464 | tf_op jit(solution)/shard_map/ppermute | solution.py:528
  3.1 3.4 %collective-permute-start.3 = (f32[16,128]{1,0:T(8,128)S(1)}, f32[16,128]{1,0:T(8,128)S(1)}, u32[]{:S(2)}, u32[]{:S(2)}) collective-permute-start(f32[16,128]{1,0:T(8,128)S(1)} %get-tuple-element.17), channel_id=1, source_target_pairs={{0,1},{1,0},{2,4},{3,5},{4,2},{5,3},{6,8},{7,9},{8,6},{9,7},{10,12... | collective-permute-start | bytes 24584 | tf_op jit(solution)/shard_map/ppermute | solution.py:528
  6.5 0.0 collective-permute-start.2
  6.5 2.4 %collective-permute-done.3.fd = f32[16,128]{1,0:T(8,128)S(1)} collective-permute-done((f32[16,128]{1,0:T(8,128)S(1)}, f32[16,128]{1,0:T(8,128)S(1)}, u32[]{:S(2)}, u32[]{:S(2)}) %collective-permute-start.3) | collective-permute-done | bytes 8224 | tf_op jit(solution)/shard_map/ppermute | solution.py:528
  8.8 1.3 %collective-permute-done.2.fc = f32[16,128]{1,0:T(8,128)S(1)} collective-permute-done((f32[16,128]{1,0:T(8,128)S(1)}, f32[16,128]{1,0:T(8,128)S(1)}, u32[]{:S(2)}, u32[]{:S(2)}) %collective-permute-start.2) | collective-permute-done | bytes 8224 | tf_op jit(solution)/shard_map/ppermute | solution.py:528
  10.1 0.0 collective-permute-done.ha
  10.1 0.0 collective-permute-done.1.hb
  10.1 0.0 copy-done.1
  10.1 0.0 copy-done
  10.1 1.3 %extend_z.1 = (f32[144,128]{1,0:T(8,128)S(1)}, f32[144,128]{1,0:T(8,128)S(1)}, f32[64,128]{1,0:T(8,128)S(1)}, f32[16,16,128]{2,1,0:T(8,128)S(1)}, f32[64,128]{1,0:T(8,128)S(1)}, /*index=5*/f32[64,128]{1,0:T(8,128)S(1)}) custom-call(f32[32,32,128]{2,1,0:T(8,128)S(1)} %get-tuple-element.13.fine, s32[2,2,8]{2,1,0:T(2,128)S(1)} %copy-done.1, ...), custom_call_target="tpu_custom_call" | custom-call | tf_op jit(solution)/shard_map/extend_z/pallas_call | solution.py:556
  11.5 1.6 %collective-permute-start.4 = (f32[144,128]{1,0:T(8,128)S(1)}, f32[144,128]{1,0:T(8,128)S(1)}, u32[]{:S(2)}, u32[]{:S(2)}) collective-permute-start(f32[144,128]{1,0:T(8,128)S(1)} %get-tuple-element.18), channel_id=1, source_target_pairs={{0,32},{1,33},{2,34},{3,35},{4,36},{5,37},{6,38},{7,39},{8,40},{9,... | collective-permute-start | bytes 221192 | tf_op jit(solution)/shard_map/ppermute | solution.py:528
  13.1 2.8 %collective-permute-start.5 = (f32[144,128]{1,0:T(8,128)S(1)}, f32[144,128]{1,0:T(8,128)S(1)}, u32[]{:S(2)}, u32[]{:S(2)}) collective-permute-start(f32[144,128]{1,0:T(8,128)S(1)} %get-tuple-element.19), channel_id=1, source_target_pairs={{0,1},{1,0},{2,3},{3,2},{4,5},{5,4},{6,7},{7,6},{8,9},{9,8},{10,11... | collective-permute-start | bytes 221192 | tf_op jit(solution)/shard_map/ppermute | solution.py:528
  15.8 0.2 collective-permute-done.4.xa
  16.0 5.0 %collective-permute-done.5.xb = f32[144,128]{1,0:T(8,128)S(1)} collective-permute-done((f32[144,128]{1,0:T(8,128)S(1)}, f32[144,128]{1,0:T(8,128)S(1)}, u32[]{:S(2)}, u32[]{:S(2)}) %collective-permute-start.5) | collective-permute-done | bytes 73760 | tf_op jit(solution)/shard_map/ppermute | solution.py:528
  21.0 4.2 %sweep_all.1 = (f32[16,16,64]{2,1,0:T(8,128)}, f32[32,32,128]{2,1,0:T(8,128)}) custom-call(f32[32,32,128]{2,1,0:T(8,128)S(1)} %get-tuple-element.13.fine, f32[144,128]{1,0:T(8,128)S(1)} %collective-permute-done.4.xa, f32[144,128]{1,0:T(8,128)S(1)} %collective-permute-done.5.xb, f32[64,128]{1,0:T(8,128)S(1)} %get-tuple-element.20.start, ...), custom_call_target="tpu_custom_call" | custom-call | tf_op jit(solution)/shard_map/sweep_all/pallas_call | solution.py:578
Async XLA Ops:
  0.6 9.5 %copy-start.1 = (s32[2,2,8]{2,1,0:T(2,128)S(1)}, s32[2,2,8]{2,1,0:T(2,128)}, u32[]{:S(2)}) copy-start(s32[2,2,8]{2,1,0:T(2,128)} %par.1) | copy-start | bytes 388
  2.1 8.0 %copy-start = (f32[1,4,512]{2,1,0:T(4,128)S(1)}, f32[1,4,512]{2,1,0:T(4,128)}, u32[]{:S(2)}) copy-start(f32[1,4,512]{2,1,0:T(4,128)} %co.1) | copy-start | bytes 24580
  2.1 8.0 %collective-permute-start = (f32[96,128]{1,0:T(8,128)S(1)}, f32[96,128]{1,0:T(8,128)S(1)}, u32[]{:S(2)}, u32[]{:S(2)}) collective-permute-start(f32[96,128]{1,0:T(8,128)S(1)} %get-tuple-element.15), channel_id=1, source_target_pairs={{0,1},{1,0},{2,3},{3,2},{4,5},{5,4},{6,7},{7,6},{8,9},{9,8},{10,11... | collective-permute-start | bytes 147464 | tf_op jit(solution)/shard_map/ppermute | solution.py:528
  2.2 7.9 %collective-permute-start.1 = (f32[96,128]{1,0:T(8,128)S(1)}, f32[96,128]{1,0:T(8,128)S(1)}, u32[]{:S(2)}, u32[]{:S(2)}) collective-permute-start(f32[96,128]{1,0:T(8,128)S(1)} %get-tuple-element.16), channel_id=1, source_target_pairs={{0,32},{1,2},{2,1},{3,4},{4,3},{5,6},{6,5},{7,8},{8,7},{9,10},{10,... | collective-permute-start | bytes 147464 | tf_op jit(solution)/shard_map/ppermute | solution.py:528
  3.1 5.8 %collective-permute-start.3 = (f32[16,128]{1,0:T(8,128)S(1)}, f32[16,128]{1,0:T(8,128)S(1)}, u32[]{:S(2)}, u32[]{:S(2)}) collective-permute-start(f32[16,128]{1,0:T(8,128)S(1)} %get-tuple-element.17), channel_id=1, source_target_pairs={{0,1},{1,0},{2,4},{3,5},{4,2},{5,3},{6,8},{7,9},{8,6},{9,7},{10,12... | collective-permute-start | bytes 24584 | tf_op jit(solution)/shard_map/ppermute | solution.py:528
  6.5 3.7 %collective-permute-start.2 = (f32[16,128]{1,0:T(8,128)S(1)}, f32[16,128]{1,0:T(8,128)S(1)}, u32[]{:S(2)}, u32[]{:S(2)}) collective-permute-start(f32[16,128]{1,0:T(8,128)S(1)} %get-tuple-element.17), channel_id=1, source_target_pairs={{0,2},{1,3},{2,0},{3,1},{4,6},{5,7},{6,4},{7,5},{8,10},{9,11},{10,... | collective-permute-start | bytes 24584 | tf_op jit(solution)/shard_map/ppermute | solution.py:528
  11.5 4.5 %collective-permute-start.4 = (f32[144,128]{1,0:T(8,128)S(1)}, f32[144,128]{1,0:T(8,128)S(1)}, u32[]{:S(2)}, u32[]{:S(2)}) collective-permute-start(f32[144,128]{1,0:T(8,128)S(1)} %get-tuple-element.18), channel_id=1, source_target_pairs={{0,32},{1,33},{2,34},{3,35},{4,36},{5,37},{6,38},{7,39},{8,40},{9,... | collective-permute-start | bytes 221192 | tf_op jit(solution)/shard_map/ppermute | solution.py:528
  13.1 8.0 %collective-permute-start.5 = (f32[144,128]{1,0:T(8,128)S(1)}, f32[144,128]{1,0:T(8,128)S(1)}, u32[]{:S(2)}, u32[]{:S(2)}) collective-permute-start(f32[144,128]{1,0:T(8,128)S(1)} %get-tuple-element.19), channel_id=1, source_target_pairs={{0,1},{1,0},{2,3},{3,2},{4,5},{5,4},{6,7},{7,6},{8,9},{9,8},{10,11... | collective-permute-start | bytes 221192 | tf_op jit(solution)/shard_map/ppermute | solution.py:528
